TPU v7x, 256 devices: a whole 4x4x8 slice. The times are simulated.
256 devices in a mesh: tp: 16 (over z_lo, y), dp: 16 (over z_hi, x, core).
Axes of the slice: x: 4, y: 4, z: 8 (z_hi: 2, z_lo: 4; z = z_hi * 4 + z_lo), core: 2. Of those that a mesh axis runs over, the one named last changes fastest.
Arguments:
- normed: bfloat16 [8192, 4096], P(('dp', 'tp')), may hold values from -6 to 6
- cotangent: bfloat16 [8192, 8192], P('dp', 'tp'), may hold values from -0.52734375 to 0.52734375
- weight_tiles: bfloat16 [2, 2048, 128, 128], P(None, 'tp'), may hold values from -0.09375 to 0.09375
- slot_tile: int32 [2048], replicated, may hold values from 0 to 2047, as said below
Outputs:
- hidden: bfloat16 [8192, 8192], P('dp', 'tp')
- d_normed: bfloat16 [8192, 4096], P(('dp', 'tp'))
- grad_tiles: float32 [2, 2048, 128, 128], P(None, 'tp', 'dp')
Inputs may be any that keep to these rules, and one draw needn't show every extreme that they name: `slot_tile`: A permutation of 0 to 2047. Position p belongs to owner p // 128 at slot p % 128. Each owner holds 6 to 10 tiles of the tile columns t * 4 to (t + 1) * 4 - 1 of each index t of tp; in every draw some owner holds exactly 10 for some t.
All inputs are finite; a program needn't handle non-finite values.
Results may differ from a plain program's by a relative error of at most 0.018.
Values may be sent and summed in bfloat16 or wider, within the bound.
A program may use at most 128 MiB of HBM per device.

v0:
```python
import jax
import jax.numpy as jnp
from jax import lax
from jax.sharding import Mesh
from jax.sharding import PartitionSpec as P

D = 4096
FW = 8192
TILE = 128
TP = ("tp_0", "tp_1")
DP_TP = ("dp", "tp_0", "tp_1")


def joined_along(tiles, dim):
    dims = list(tiles.shape[1:])
    dims[dim] *= tiles.shape[0]
    return jnp.moveaxis(tiles, 0, dim).reshape(dims)


def all_blocks(array, axes, order):
    tiles = array
    for k in order:
        tiles = lax.all_gather(tiles, axes[k])
    done = order[::-1]
    back = [done.index(k) for k in range(len(axes))]
    tiles = tiles.transpose(*back, *range(len(axes), tiles.ndim))
    return tiles.reshape(-1, *array.shape)


def whole_of(array, axes, order, dim):
    return joined_along(all_blocks(array, axes, order), dim)


def own_block(tiles, axes, order):
    inside = tiles.shape[1:]
    tiles = tiles.reshape(*(lax.axis_size(a) for a in axes), *inside)
    tiles = jnp.moveaxis(tiles, order, range(len(axes))).reshape(-1, *inside)
    for k in order:
        tiles = lax.psum_scatter(tiles, axes[k], scatter_dimension=0, tiled=True)
    return tiles[0]


def cut_along(array, dim, count):
    before, after = (array.shape[:dim], array.shape[dim + 1 :])
    return jnp.moveaxis(array.reshape(*before, count, -1, *after), dim, 0)


def sum_by_axis(array, axes, order, dim):
    count = lax.axis_size(axes)
    return own_block(cut_along(array, dim, count), axes, order)


def build_lists(slot_tile, groups, owned_count, tile_cols, cols_dev, list_len):
    owned_tiles = slot_tile.reshape(groups, owned_count)
    target = owned_tiles % tile_cols // cols_dev
    matches = (target[:, :, None] == jnp.arange(groups, dtype=jnp.int32)[None, None, :]).astype(
        jnp.int32
    )
    running = jnp.cumsum(matches, axis=1) - 1
    rank_of = jnp.sum(running * matches, axis=2)
    owner_ix = jnp.broadcast_to(jnp.arange(groups, dtype=jnp.int32)[:, None], (groups, owned_count))
    slot_ix = jnp.broadcast_to(
        jnp.arange(owned_count, dtype=jnp.int32)[None, :], (groups, owned_count)
    )
    table = jnp.full((groups, groups, list_len), -1, jnp.int32)
    return table.at[owner_ix, target, rank_of].set(slot_ix, mode="drop")


def incoming_places(in_lists, slot_tile, consumer, tile_cols, cols_dev, owned_count):
    groups = in_lists.shape[0]
    present = in_lists >= 0
    position = jnp.arange(groups, dtype=jnp.int32)[:, None] * owned_count + jnp.maximum(in_lists, 0)
    tile_id = slot_tile[position]
    tile_row = tile_id // tile_cols
    tile_col = tile_id % tile_cols - consumer * cols_dev
    local_idx = tile_row * cols_dev + tile_col
    return (jnp.where(present, local_idx, owned_count), present)


def pick_tiles(source, indices, present):
    limit = source.shape[1] - 1
    picked = source[:, jnp.minimum(indices, limit)]
    mask = present.reshape((1,) + present.shape + (1,) * (source.ndim - 2))
    return jnp.where(mask, picked, jnp.zeros((), source.dtype))


def place_tiles(arrived, places, owned_count):
    flat = arrived.reshape((arrived.shape[0], -1) + arrived.shape[3:])
    empty = jnp.zeros((arrived.shape[0], owned_count) + arrived.shape[3:], arrived.dtype)
    return empty.at[:, places.reshape(-1)].set(flat, mode="drop")


def local(normed, cotangent, weight_tiles, slot_tile):
    tp_size = lax.axis_size(TP)
    consumer = lax.axis_index(TP)
    owned_count = weight_tiles.shape[1]
    tile_size = weight_tiles.shape[2]
    tile_rows = D // TILE
    tile_cols = FW // TILE
    cols_dev = tile_cols // tp_size
    base_count = owned_count // tp_size
    list_len = base_count + base_count // 4
    send_lists = build_lists(slot_tile, tp_size, owned_count, tile_cols, cols_dev, list_len)
    my_lists = lax.dynamic_index_in_dim(send_lists, consumer, 0, keepdims=False)
    out_present = my_lists >= 0
    out_places = jnp.where(out_present, my_lists, owned_count)
    in_lists = lax.dynamic_index_in_dim(send_lists, consumer, 1, keepdims=False)
    in_places, in_present = incoming_places(
        in_lists, slot_tile, consumer, tile_cols, cols_dev, owned_count
    )
    slab_rows = tile_size // lax.axis_size("dp")
    slab_start = lax.axis_index("dp") * slab_rows
    own_rows = lax.dynamic_slice_in_dim(weight_tiles, slab_start, slab_rows, 2)
    outgoing = pick_tiles(own_rows, my_lists, out_present)
    arrived = lax.all_to_all(outgoing, TP, split_axis=1, concat_axis=1, tiled=True)
    partial_tiles = place_tiles(arrived, in_places, owned_count)
    weight_block = lax.all_gather(partial_tiles, "dp", axis=2, tiled=True)
    weight_block = weight_block.reshape(2, tile_rows, cols_dev, tile_size, tile_size)
    gathered = whole_of(normed, TP, (0, 1), 0)
    group_rows = gathered.shape[0]
    tiled_in = gathered.reshape(group_rows, tile_rows, tile_size)
    both_proj = jnp.einsum(
        "nri,mrcij->nmcj", tiled_in, weight_block, preferred_element_type=jnp.float32
    )
    gate_proj = both_proj[:, 0].reshape(group_rows, -1)
    up_proj = both_proj[:, 1].reshape(group_rows, -1)
    sigmoid_gate = jax.nn.sigmoid(gate_proj)
    act_gate = gate_proj * sigmoid_gate
    hidden = (act_gate * up_proj).astype(jnp.bfloat16)
    cot_full = cotangent.astype(jnp.float32)
    grad_gate = (
        cot_full * up_proj * (sigmoid_gate * (1.0 + gate_proj * (1.0 - sigmoid_gate)))
    ).astype(jnp.bfloat16)
    grad_up = (cot_full * act_gate).astype(jnp.bfloat16)
    grads_in = jnp.stack([grad_gate, grad_up], 1).reshape(group_rows, 2, cols_dev, tile_size)
    term = jnp.einsum("nmcj,mrcij->nri", grads_in, weight_block, preferred_element_type=jnp.float32)
    d_normed = (
        sum_by_axis(
            term.reshape(normed.shape[0] * lax.axis_size(TP), -1).astype(jnp.bfloat16),
            TP,
            (1, 0),
            0,
        )
        .astype(jnp.float32)
        .astype(jnp.bfloat16)
    )
    partial_value = jnp.einsum(
        "nri,nmcj->mrcij", tiled_in, grads_in, preferred_element_type=jnp.float32
    ).astype(jnp.bfloat16)
    partial_value = partial_value.reshape(2, owned_count, tile_size, tile_size)
    summed = lax.psum_scatter(partial_value, "dp", scatter_dimension=2, tiled=True).astype(
        jnp.float32
    )
    outgoing_grads = pick_tiles(summed, in_places, in_present)
    returned = lax.all_to_all(
        outgoing_grads.astype(jnp.bfloat16), TP, split_axis=1, concat_axis=1, tiled=True
    ).astype(outgoing_grads.dtype)
    result = place_tiles(returned, out_places, owned_count)
    return (hidden, d_normed, result)


def solution(mesh):
    finer = Mesh(mesh.devices.reshape(4, 4, mesh.shape["dp"]), ("tp_0", "tp_1", "dp"))
    placed = (P(DP_TP, None), P("dp", TP), P(None, TP, None, None), P())
    return jax.shard_map(
        local,
        mesh=finer,
        in_specs=placed,
        out_specs=(P("dp", TP), P(DP_TP, None), P(None, TP, "dp", None)),
        check_vma=False,
    )
```

profile of v0, /device:TPU:1, one launch (start us, length us, event | category | flops | bytes accessed | tf_op | source)
XLA Modules:
  0.0 490.6 jit_solution(926852536485832651)
XLA Ops:
  7.2 0.7 all-gather.8.cloned.1.call-update
  8.0 38.4 %all-gather.8.cloned.1.call-done = bf16[128,4096]{1,0:T(8,128)(2,1)} async-done(((bf16[32,4096]{1,0:T(8,128)(2,1)}), bf16[128,4096]{1,0:T(8,128)(2,1)}) %all-gather.8.cloned.1.call-update) | async-done | bytes 1048592 | tf_op jit(solution)/shard_map/all_gather | solution.py:23
  46.4 0.7 add_select_fusion
  47.1 0.1 copy.92
  47.2 2.8 select_reduce_fusion
  50.1 0.7 compare_select_fusion.3
  50.8 0.7 multiply_reduce_fusion
  51.6 0.7 and_reduce_fusion
  52.3 8.1 %scatter_custom_fusion.2 = s32[2560]{0:T(1024)S(1)} fusion(s32[2048]{0:T(1024)S(1)} %select_bitcast_fusion.1, s32[2048]{0:T(1024)S(1)} %iota_bitcast_fusion, s32[]{:T(128)} %constant.88.clone.1), kind=kCustom, calls=%fused_computation.81 | custom fusion | bytes 10244
  60.4 0.1 reshape.536
  60.5 0.1 copy.97
  60.6 0.1 reshape.550
  60.7 0.1 copy.96
  60.8 1.1 constant_dynamic-slice_fusion
  61.9 0.8 gather_fusion.1
  62.7 1.1 select_bitcast_fusion
  63.8 4.8 all-to-all-start
  68.7 0.1 compare_bitcast_fusion
  68.8 0.2 copy.94
  69.0 0.1 ge.52
  69.1 0.3 bitcast_reduce_fusion
  69.5 0.1 copy.95
  69.5 0.1 reshape.542
  69.7 1.4 gather_fusion
  71.1 13.0 %all-to-all-done = bf16[2,16,10,8,128]{4,3,0,2,1:T(8,128)(2,1)S(1)} async-done(((bf16[2,16,10,8,128]{4,3,0,2,1:T(8,128)(2,1)}), bf16[2,16,10,8,128]{4,3,0,2,1:T(8,128)(2,1)S(1)}, u32[]{:S(2)}, u32[]{:S(2)}) %all-to-all-start) | async-done | bytes 655392 | tf_op jit(solution)/shard_map/all_to_all | solution.py:115
  84.2 6.9 %scatter_fusion = bf16[2,128,8,128]{3,2,1,0:T(8,128)(2,1)S(1)} fusion(bf16[2,128,8,128]{3,2,1,0:T(8,128)(2,1)S(1)} %broadcast_in_dim.63, s32[160]{0:T(256)S(1)} %bitcast.163, bf16[160,2,8,128]{3,2,1,0:T(8,128)(2,1)S(1)} %bitcast.151), kind=kCustom, calls=%fused_computation.3 | custom fusion | bytes 1966720 | tf_op jit(solution)/shard_map/scatter | solution.py:90
  91.1 0.8 copy-done.1
  91.9 0.2 reduce-scatter.6.cloned.1.call-start
  92.2 0.2 copy.101
  92.4 13.2 %all-gather.10.cloned.1.call-done = bf16[16,32,4096]{2,1,0:T(8,128)(2,1)} async-done(((bf16[4,32,4096]{2,1,0:T(8,128)(2,1)}), bf16[16,32,4096]{2,1,0:T(8,128)(2,1)}) %all-gather.10.cloned.1.call-update) | async-done | bytes 4194320 | tf_op jit(solution)/shard_map/all_gather | solution.py:23
  105.6 2.5 copy.98
  108.0 3.2 copy.134
  111.2 111.1 %all-gather.6.cloned.1.call-done = bf16[2,128,128,128]{3,2,1,0:T(8,128)(2,1)} async-done(((bf16[2,128,8,128]{3,2,1,0:T(8,128)(2,1)}), bf16[2,128,128,128]{3,2,1,0:T(8,128)(2,1)}) %all-gather.6.cloned.1.call-update) | async-done | bytes 8388624 | tf_op jit(solution)/shard_map/all_gather | solution.py:117
  222.3 10.6 %fusion.4 = f32[512,2,4,128]{0,3,2,1:T(8,128)S(1)} fusion(bf16[2,32,4,128,128]{4,3,2,1,0:T(8,128)(2,1)} %bitcast.144, bf16[512,32,128,1,1]{2,1,0,4,3:T(8,128)(2,1)} %bitcast.148), kind=kOutput, calls=%fused_computation.13 | convolution fusion | flops 4294967296 | bytes 14680064 | tf_op jit(solution)/shard_map/nri,mrcij->nmcj/dot_general | solution.py:122
  232.9 0.2 fusion.37
  233.1 10.3 %copy.104 = bf16[32,128,4,128,2]{3,1,0,4,2:T(8,128)(2,1)} copy(bf16[32,128,4,128,2]{3,1,2,0,4:T(8,128)(2,1)} %bitcast.145) | data formatting | bytes 16777216 | tf_op jit(solution)/shard_map/nmcj,mrcij->nri/dot_general | solution.py:136
  243.4 0.7 fusion.8
  244.1 0.3 copy.103
  244.3 0.3 copy.102
  244.6 8.2 %bitcast_convert_fusion = bf16[512,4096]{1,0:T(8,128)(2,1)S(1)} fusion(bf16[4096,4,128,2]{2,0,3,1:T(8,128)(2,1)} %bitcast.146, bf16[512,1,4,128]{3,0,1,2:T(8,128)(2,1)S(1)} %copy.103, bf16[512,1,4,128]{3,0,1,2:T(8,128)(2,1)S(1)} %copy.102), kind=kOutput, calls=%fused_computation.7 | convolution fusion | flops 4297588736 | bytes 13631488 | tf_op jit(solution)/shard_map/nmcj,mrcij->nri/dot_general | solution.py:136
  252.8 2.5 copy.105
  255.3 9.5 %convert_bitcast_fusion = bf16[2,32,4,128,128]{3,4,1,2,0:T(8,128)(2,1)} fusion(bf16[512,32,128,1,1]{2,1,0,4,3:T(8,128)(2,1)} %bitcast.149, bf16[512,1,4,128]{3,0,1,2:T(8,128)(2,1)S(1)} %copy.103, bf16[512,1,4,128]{3,0,1,2:T(8,128)(2,1)S(1)} %copy.102), kind=kOutput, calls=%fused_computation.8 | convolution fusion | flops 4299685888 | bytes 13631488 | tf_op jit(solution)/shard_map/nri,nmcj->mrcij/dot_general | solution.py:147
  264.9 12.0 %copy.110 = bf16[2,32,4,128,128]{4,3,2,1,0:T(8,128)(2,1)} copy(bf16[2,32,4,128,128]{3,4,1,2,0:T(8,128)(2,1)} %convert_bitcast_fusion) | data formatting | bytes 16777216 | tf_op jit(solution)/shard_map/convert_element_type | solution.py:149
  276.9 12.0 %copy.132 = bf16[2,128,128,128]{3,1,0,2:T(8,128)(2,1)} copy(bf16[2,128,128,128]{3,2,1,0:T(8,128)(2,1)} %bitcast.140) | data formatting | bytes 16777216
  288.9 14.0 %copy.150 = bf16[16,8,256,128]{3,1,2,0:T(8,128)(2,1)} copy(bf16[16,8,256,128]{3,2,1,0:T(8,128)(2,1)} %bitcast.141) | data formatting | bytes 16777216
  303.0 0.1 gather.16
  303.1 0.1 copy.116
  303.2 0.1 copy.112
  303.3 0.2 reduce-scatter.8.cloned.1.call-update
  303.6 0.1 copy.117
  303.7 0.1 reshape.558
  303.8 138.6 %reduce-scatter.10.cloned.1.call-done = bf16[8,32768]{1,0:T(8,128)(2,1)} async-done(((bf16[128,32768]{1,0:T(8,128)(2,1)}), bf16[8,32768]{1,0:T(8,128)(2,1)}) %reduce-scatter.10.cloned.1.call-update) | async-done | bytes 524304
  442.4 1.1 copy.136
  443.5 0.3 copy.149
  443.8 0.8 gather_fusion.2
  444.6 1.1 fusion.20
  445.7 4.7 all-to-all-start.1
  450.5 0.1 copy.106
  450.5 0.1 squeeze.10
  450.6 1.0 copy.118
  451.6 18.1 %all-to-all-done.1 = bf16[2,16,10,8,128]{4,3,0,2,1:T(8,128)(2,1)S(1)} async-done(((bf16[2,16,10,8,128]{4,3,0,2,1:T(8,128)(2,1)}), bf16[2,16,10,8,128]{4,3,0,2,1:T(8,128)(2,1)S(1)}, u32[]{:S(2)}, u32[]{:S(2)}) %all-to-all-start.1) | async-done | bytes 655392 | tf_op jit(solution)/shard_map/all_to_all | solution.py:155
  469.8 0.1 convert_bitcast_fusion.1
  470.0 6.8 %scatter_fusion.1 = f32[2,128,8,128]{3,2,1,0:T(8,128)S(1)} fusion(f32[2,128,8,128]{3,2,1,0:T(8,128)S(1)} %broadcast_in_dim.71, s32[160]{0:T(256)S(1)} %bitcast.164, f32[160,2,8,128]{3,2,1,0:T(8,128)S(1)} %convert_bitcast_fusion.1), kind=kCustom, calls=%fused_computation.4 | custom fusion | bytes 3932800 | tf_op jit(solution)/shard_map/scatter | solution.py:90
  476.8 6.9 %reduce-scatter.8.cloned.1.call-done = bf16[1,32,4096]{2,1,0:T(8,128)(2,1)} async-done(((bf16[4,32,4096]{2,1,0:T(8,128)(2,1)}), bf16[1,32,4096]{2,1,0:T(8,128)(2,1)}) %reduce-scatter.8.cloned.1.call-update) | async-done | bytes 262160 | tf_op jit(solution)/shard_map/reduce_scatter | solution.py:39
  (33 shorter events, 0.6 us)
Async XLA Ops:
  7.2 62.5 %copy-start = (s32[2048]{0:T(1024)S(1)}, s32[2048]{0:T(1024)}, u32[]{:S(2)}) copy-start(s32[2048]{0:T(1024)} %param.7) | copy-start | bytes 24580
  7.2 39.2 %all-gather.8.cloned.1.call-start = ((), (), s32[]{:S(2)}) async-start(), calls=%async_computation.8 | async-start | bytes 1310720 | tf_op jit(solution)/shard_map/all_gather | solution.py:23
  7.9 97.7 %all-gather.10.cloned.1.call-start = ((), (), s32[]{:S(2)}) async-start(), calls=%async_computation.9 | async-start | bytes 5242880 | tf_op jit(solution)/shard_map/all_gather | solution.py:23
  63.8 20.3 %all-to-all-start = ((bf16[2,16,10,8,128]{4,3,0,2,1:T(8,128)(2,1)}), bf16[2,16,10,8,128]{4,3,0,2,1:T(8,128)(2,1)S(1)}, u32[]{:S(2)}, u32[]{:S(2)}) async-start(bf16[2,16,10,8,128]{4,3,0,2,1:T(8,128)(2,1)} %select_bitcast_fusion), calls=%async_computation | async-start | bytes 1310720 | tf_op jit(solution)/shard_map/all_to_all | solution.py:115
  68.6 153.7 %all-gather.6.cloned.1.call-start = ((), (), s32[]{:S(2)}) async-start(), calls=%async_computation.5 | async-start | bytes 8912896 | tf_op jit(solution)/shard_map/all_gather | solution.py:117
  69.7 22.5 %copy-start.3 = (bf16[512,512]{1,0:T(8,128)(2,1)S(1)}, bf16[512,512]{1,0:T(8,128)(2,1)}, u32[]{:S(2)}) copy-start(bf16[512,512]{1,0:T(8,128)(2,1)} %param.5) | copy-start | bytes 1572868
  91.1 0.8 copy-start.1
  91.9 211.4 %reduce-scatter.6.cloned.1.call-start = ((), (), s32[]{:S(2)}) async-start(), calls=%async_computation.6 | async-start | bytes 5242880 | tf_op jit(solution)/shard_map/reduce_scatter | solution.py:39
  255.3 187.1 %reduce-scatter.10.cloned.1.call-start = ((), (), s32[]{:S(2)}) async-start(), calls=%async_computation.10 | async-start | bytes 8912896
  302.9 180.8 %reduce-scatter.8.cloned.1.call-start = ((), (), s32[]{:S(2)}) async-start(), calls=%async_computation.7 | async-start | bytes 1310720 | tf_op jit(solution)/shard_map/reduce_scatter | solution.py:39
  445.7 24.1 %all-to-all-start.1 = ((bf16[2,16,10,8,128]{4,3,0,2,1:T(8,128)(2,1)}), bf16[2,16,10,8,128]{4,3,0,2,1:T(8,128)(2,1)S(1)}, u32[]{:S(2)}, u32[]{:S(2)}) async-start(bf16[2,16,10,8,128]{4,3,0,2,1:T(8,128)(2,1)} %fusion.20), calls=%async_computation.3 | async-start | bytes 1310720 | tf_op jit(solution)/shard_map/all_to_all | solution.py:155
  476.8 6.9 %copy-start.2 = (f32[2,128,8,128]{3,2,1,0:T(8,128)}, f32[2,128,8,128]{3,2,1,0:T(8,128)S(1)}, u32[]{:S(2)}) copy-start(f32[2,128,8,128]{3,2,1,0:T(8,128)S(1)} %scatter_fusion.1) | copy-start | bytes 3145732
Sparse Core Ops, SparseCore 0:
  9.8 36.5 all-gather.7
  48.2 57.3 all-gather.9
  108.7 113.5 all-gather.5
  255.4 44.2 reduce-scatter.5
  304.2 138.1 reduce-scatter.9
  445.3 38.3 reduce-scatter.7
where the time goes:
time: 498 us; the launch traced here: 491 us
  waiting for transfers between devices  340 us (68%)
  local copies, waits for them, and re-layouts  88.3 us (18%)
  matrix products  28.3 us (6%)
  between operations  14.4 us (3%)
  starting transfers between devices  9.98 us (2%)
  other arithmetic  9.23 us (2%)
    unnamed x7, waiting for transfers between devices  140 us
    all_gather x1, waiting for transfers between devices, local(): weight_block = lax.all_gather(partial_tiles, 'dp', axis=2, tiled=True)  111 us
    all_gather x2, waiting for transfers between devices, all_blocks(): tiles = lax.all_gather(tiles, axes[k])  51.6 us
    unnamed x17, local copies, waits for them, and re-layouts  40.9 us
    all_to_all x1, waiting for transfers between devices, local(): lax.all_to_all(outgoing_grads.astype(jnp.bfloat16), TP, split_axis=1, con...  18.1 us
    scatter x2, local copies, waits for them, and re-layouts, place_tiles(): return empty.at[:, places.reshape(-1)].set(flat, mode='drop')  13.7 us
    all_to_all x1, waiting for transfers between devices, local(): lax.all_to_all(outgoing, TP, split_axis=1, concat_axis=1, tiled=True)  13 us
    convert_element_type x1, local copies, waits for them, and re-layouts, local(): partial_value = jnp.einsum('nri,nmcj->mrcij', tiled_in, grads_in, preferr...  12 us
  transfers between devices with their start and end apart: 8, of which 7 were waited for; matrix products, arithmetic and copies ran while one was open for 19% of the time, Pallas kernels for 0%

commit v1 on v0

v1 whole, which is shorter than its diff:
```python
import jax
import jax.numpy as jnp
from jax import lax
from jax.experimental import pallas as pl
from jax.experimental.pallas import tpu as pltpu
from jax.sharding import Mesh
from jax.sharding import PartitionSpec as P

D = 4096
FW = 8192
TILE = 128
TC = FW // TILE
OWNERS = 16
OWN = 128
CPD = TC // OWNERS
RANKS = 10
TOK = 32
GROUP = 512
AXES = ("zl", "y", "zh", "x", "c")
MESH = pl.DeviceIdType.MESH
BF = jnp.bfloat16
F32 = jnp.float32
DZ = (1, 7, 2, 6, 0)


def index_lists(slot_tile, me):
    tiles = slot_tile.reshape(OWNERS, OWN)
    target = tiles % TC // CPD
    seq = jnp.arange(OWN, dtype=jnp.int32)
    ahead = seq[None, None, :] < seq[None, :, None]
    same = target[:, :, None] == target[:, None, :]
    rank = jnp.sum((same & ahead).astype(jnp.int32), axis=2)
    owners = jnp.arange(OWNERS, dtype=jnp.int32)
    ranks = jnp.arange(RANKS, dtype=jnp.int32)
    my_target = lax.dynamic_index_in_dim(target, me, 0, keepdims=False)
    my_rank = lax.dynamic_index_in_dim(rank, me, 0, keepdims=False)
    my_code = my_target * RANKS + my_rank
    codes = jnp.arange(OWNERS * RANKS, dtype=jnp.int32)
    pick = jnp.sum(jnp.where(my_code[None, :] == codes[:, None], seq[None, :], 0), axis=1)
    mine = target == me
    place = tiles // TC * CPD + tiles % TC - me * CPD
    source = owners[:, None] * RANKS + rank
    inverse = jnp.sum(
        jnp.where(mine[None] & (place[None] == seq[:, None, None]), source[None], 0), axis=(1, 2)
    )
    grad_pick = jnp.sum(
        jnp.where(mine[:, None, :] & (rank[:, None, :] == ranks[None, :, None]), place[:, None, :], 0),
        axis=2,
    ).reshape(-1)
    return pick, inverse, grad_pick, my_code


def kernel(
    pick_ref, inv_ref, gpick_ref, ginv_ref, tok_hbm, cot_hbm, own_hbm,
    hid_hbm, dn_hbm, gt_hbm,
    own, outg, arrv, xs, ws, cot, hid, acc, grads, term, yfar, ynear, zrecv, dnout,
    part, precv, xfar, xnear, fsum, gout, garr, give, gres,
    ld, a_s, a_r, tz_s, tz_r, tn_s, tn_r, tf_s, tf_r, wn_s, wn_r, wf_s, wf_r, wd_s, wd_r,
    pd_s, pd_r, xf_s, xf_r, xn_s, xn_r, yf_s, yf_r, yn_s, yn_r, zr_s, zr_r, g_s, g_r, q_s, q_r,
):
    zl, y, zh, x, c = (lax.axis_index(a) for a in AXES)
    z = zh * 4 + zl
    me = zl * 4 + y

    def dev(dz=0, dy=0, dx=0, dc=0):
        zz = lax.rem(z + dz, 8)
        return (
            lax.rem(zz, 4), lax.rem(y + dy, 4), lax.div(zz, 4), lax.rem(x + dx, 4), lax.rem(c + dc, 2),
        )

    def rcopy(src, dst, ss, rs, to):
        return pltpu.make_async_remote_copy(
            src_ref=src, dst_ref=dst, send_sem=ss, recv_sem=rs, device_id=to, device_id_type=MESH
        )

    sends = []

    def send(src, dst, ss, rs, to):
        copy = rcopy(src, dst, ss, rs, to)
        copy.start()
        sends.append(copy)

    def recv(dst, ss, rs):
        rcopy(dst, dst, ss, rs, dev(dc=1)).wait_recv()

    band = x * 2 + c
    load_own = pltpu.make_async_copy(
        own_hbm.at[:, :, pl.ds(pl.multiple_of(band * 16, 16), 16), :], own, ld.at[0]
    )
    load_own.start()
    load_tok = pltpu.make_async_copy(tok_hbm, xs.at[zl, y], ld.at[1])
    load_tok.start()
    load_cot = pltpu.make_async_copy(cot_hbm, cot, ld.at[2])
    load_cot.start()

    barrier = pltpu.get_barrier_semaphore()

    @pl.loop(1, 32)
    def _(j):
        dz, dy = lax.div(j, 4), lax.rem(j, 4)
        pl.semaphore_signal(barrier, inc=1, device_id=dev(dz, dy), device_id_type=MESH)

    for to in (dev(dx=1), dev(dx=3), dev(dc=1)):
        pl.semaphore_signal(barrier, inc=1, device_id=to, device_id_type=MESH)

    load_own.wait()

    def pick_into(dst, t):
        @pl.loop(0, RANKS)
        def _(k):
            slot = pick_ref[t * RANKS + k]
            for m in range(2):
                dst[t * RANKS + k, m] = own[m, slot]

    pick_into(arrv, me)
    pl.semaphore_wait(barrier, 34)

    def tile_message(dz, dy, ref, far_side):
        zz = lax.rem(z + (8 - dz if far_side else dz), 8)
        other = lax.rem(zz, 4) * 4 + lax.rem(y + (4 - dy if far_side else dy), 4)
        rows = pl.ds(other * RANKS, RANKS)
        if dz == 2:
            return ref.at[rows, 0]
        if dz == 6:
            return ref.at[rows, 1]
        return ref.at[rows]

    mine_rows = pl.ds(me * RANKS, RANKS)

    def landing(dz, ref):
        if dz == 2:
            return ref.at[mine_rows, 0]
        if dz == 6:
            return ref.at[mine_rows, 1]
        return ref.at[mine_rows]

    for i, dz in enumerate(DZ):
        for dy in range(4):
            if dz == 0 and dy == 0:
                continue
            if dz != 6:
                zz = lax.rem(z + dz, 8)
                pick_into(outg, lax.rem(zz, 4) * 4 + lax.rem(y + dy, 4))
            n = i * 4 + dy
            send(tile_message(dz, dy, outg, False), landing(dz, arrv), a_s.at[n], a_r.at[n], dev(dz, dy))

    load_tok.wait()
    for j in range(1, 4):
        to = (lax.rem(zl + j, 4), y, zh, x, c)
        send(xs.at[zl, y], xs.at[zl, y], tz_s.at[j - 1], tz_r.at[j - 1], to)

    def near_tokens(q):
        zq = lax.rem(zl + 4 - q, 4)
        for way, dy in ((0, 1), (1, 3)):
            send(xs.at[zq, y], xs.at[zq, y], tn_s.at[q, way], tn_r.at[q, way], dev(dy=dy))

    def far_tokens(q):
        zq = lax.rem(zl + 4 - q, 4)
        for way, dy in ((0, 1), (1, 3)):
            src = lax.rem(y + 4 - dy, 4)
            recv(xs.at[zq, src], tn_s.at[q, way], tn_r.at[q, way])
            half = pl.ds(16 * way, 16)
            send(xs.at[zq, src, half], xs.at[zq, src, half], tf_s.at[q, way], tf_r.at[q, way], dev(dy=dy))

    def last_tokens(q):
        zq, src = lax.rem(zl + 4 - q, 4), lax.rem(y + 2, 4)
        for way in range(2):
            recv(xs.at[zq, src, pl.ds(16 * way, 16)], tf_s.at[q, way], tf_r.at[q, way])

    near_tokens(0)

    for i, dz in enumerate(DZ):
        for dy in range(4):
            if dz == 0 and dy == 0:
                continue
            n = i * 4 + dy
            recv(tile_message(dz, dy, arrv, True), a_s.at[n], a_r.at[n])

    @pl.loop(0, D // TILE)
    def _(r):
        for col in range(CPD):
            src = inv_ref[r * CPD + col]
            for m in range(2):
                ws[m, r, band, :, col * TILE : (col + 1) * TILE] = arrv[src, m]

    for m in range(2):
        for way in range(2):
            mm = m if way == 0 else 1 - m
            send(
                ws.at[mm, :, band], ws.at[mm, :, band], wn_s.at[mm, way], wn_r.at[mm, way],
                dev(dx=1 if way == 0 else 3),
            )
    for m in range(2):
        send(ws.at[m, :, band], ws.at[m, :, band], wd_s.at[m], wd_r.at[m], dev(dc=1))

    for q in range(1, 4):
        recv(xs.at[lax.rem(zl + 4 - q, 4), y], tz_s.at[q - 1], tz_r.at[q - 1])
        near_tokens(q)

    far_tokens(0)

    def side_band(way, core):
        return lax.rem(x + (3 if way == 0 else 1), 4) * 2 + core

    def near_weights(m, way, n, forward):
        b = side_band(way, c)
        block = ws.at[m, :, b]
        recv(block, wn_s.at[m, way], wn_r.at[m, way])
        if forward:
            send(block, block, wf_s.at[way], wf_r.at[way], dev(dx=1 if way == 0 else 3))
        send(block, block, wd_s.at[n], wd_r.at[n], dev(dc=1))

    near_weights(0, 0, 2, True)
    near_weights(1, 1, 3, True)
    far_tokens(1)
    far_tokens(2)
    near_weights(1, 0, 4, False)
    near_weights(0, 1, 5, False)
    far_tokens(3)
    far_x = lax.rem(x + 2, 4) * 2
    for way in range(2):
        block = ws.at[way, :, far_x + c]
        recv(block, wf_s.at[way], wf_r.at[way])
        send(block, block, wd_s.at[6 + way], wd_r.at[6 + way], dev(dc=1))
    for q in range(4):
        last_tokens(q)
    other = 1 - c
    for m in range(2):
        recv(ws.at[m, :, x * 2 + other], wd_s.at[m], wd_r.at[m])
        recv(ws.at[m, :, far_x + other], wd_s.at[6 + m], wd_r.at[6 + m])
    for n, m, way in ((2, 0, 0), (3, 1, 1), (4, 1, 0), (5, 0, 1)):
        recv(ws.at[m, :, side_band(way, other)], wd_s.at[n], wd_r.at[n])

    @pl.loop(0, 4)
    def _(k):
        cols = pl.ds(pl.multiple_of(k * 1024, 1024), 1024)
        a = xs[:, :, :, cols].reshape(GROUP, 1024)
        for m in range(2):
            w = ws[m, pl.ds(k * 8, 8)].reshape(1024, GROUP)
            v = jnp.dot(a, w, preferred_element_type=F32)

            @pl.when(k == 0)
            def _():
                acc[m] = v

            @pl.when(k > 0)
            def _():
                acc[m] += v

    load_cot.wait()

    @pl.loop(0, 16)
    def _(i):
        rows = pl.ds(pl.multiple_of(i * 32, 32), 32)
        gate, up = acc[0, rows], acc[1, rows]
        s = jax.nn.sigmoid(gate)
        act = gate * s
        ct = cot[rows].astype(F32)
        hid[rows] = (act * up).astype(BF)
        grads[rows, :GROUP] = (ct * up * (s * (1.0 + gate * (1.0 - s)))).astype(BF)
        grads[rows, GROUP:] = (ct * act).astype(BF)

    store_hid = pltpu.make_async_copy(hid, hid_hbm, ld.at[3])
    store_hid.start()

    @pl.loop(0, 8)
    def _(d):
        cols = pl.ds(pl.multiple_of(d * 512, 512), 512)
        a = xs[:, :, :, cols].reshape(GROUP, 512)
        v = lax.dot_general(a, grads[...], (((0,), (0,)), ((), ())), preferred_element_type=F32)
        v = v.astype(BF).reshape(4, 2, 4, 16, 1024)
        half, row = lax.div(d, 4), lax.rem(d, 4) * 4
        for m in range(2):
            for xx in range(4):
                for col in range(CPD):
                    lo = m * GROUP + col * TILE
                    part[m, xx, half, pl.ds(row, 4), col] = v[:, :, xx, :, lo : lo + TILE]

    ring = lambda pos: (lax.rem(pos + 2, 4), lax.rem(pos + 1, 4), lax.rem(pos + 3, 4), pos)
    xt = ring(x)
    for i in range(4):
        send(part.at[other, xt[i]], precv.at[xt[i]], pd_s.at[i], pd_r.at[i], dev(dc=1))

    @pl.loop(0, 8)
    def _(d):
        v = None
        for m in range(2):
            w = ws[m, pl.ds(d * 4, 4)].reshape(GROUP, GROUP)
            g = grads[:, m * GROUP : (m + 1) * GROUP]
            t = lax.dot_general(g, w, (((1,), (1,)), ((), ())), preferred_element_type=F32)
            v = t if v is None else v + t
        v = v.astype(BF).reshape(2, 2, 4, TOK, 512)
        cols = pl.ds(pl.multiple_of(d * 512, 512), 512)
        for yy in range(4):
            term[yy, :, :, :, cols] = v[:, :, yy]

    yt = ring(y)

    def ring_far(a, t, far, ss, rs, to):
        for way in range(2):
            send(a.at[t[0], way], far.at[way], ss.at[way], rs.at[way], to[way])

    def ring_free(a, t, near, ss, rs, to):
        for way in range(2):
            h = 1 - way
            send(a.at[t[1 + way], h], near.at[way, h], ss.at[way, h], rs.at[way, h], to[way])

    def ring_sum(a, t, far, near, fs, fr, ss, rs, to, add):
        for way in range(2):
            recv(far.at[way], fs.at[way], fr.at[way])
            add(t[1 + way], way, far)
            send(a.at[t[1 + way], way], near.at[way, way], ss.at[way, way], rs.at[way, way], to[way])

    y_to = (dev(dy=1), dev(dy=3))
    x_to = (dev(dx=1), dev(dx=3))
    ring_far(term, yt, yfar, yf_s, yf_r, y_to)
    ring_free(term, yt, ynear, yn_s, yn_r, y_to)

    mine = part.at[c]

    def add_partner(t):
        for h in range(2):
            @pl.loop(0, 16)
            def _(r):
                mine[t, h, r] = (mine[t, h, r].astype(F32) + precv[t, h, r].astype(F32)).astype(BF)

    for i in range(4):
        recv(precv.at[xt[i]], pd_s.at[i], pd_r.at[i])
        add_partner(xt[i])
        if i == 0:
            ring_far(mine, xt, xfar, xf_s, xf_r, x_to)
        if i == 2:
            ring_free(mine, xt, xnear, xn_s, xn_r, x_to)

    def add_term(t, way, far):
        @pl.loop(0, 8)
        def _(i):
            cols = pl.ds(pl.multiple_of(i * 512, 512), 512)
            here = term[t, way, :, :, cols].astype(F32)
            term[t, way, :, :, cols] = (here + far[way, :, :, cols].astype(F32)).astype(BF)

    def add_part(t, way, far):
        @pl.loop(0, 16)
        def _(r):
            mine[t, way, r] = (mine[t, way, r].astype(F32) + far[way, r].astype(F32)).astype(BF)

    ring_sum(term, yt, yfar, ynear, yf_s, yf_r, yn_s, yn_r, y_to, add_term)
    ring_sum(mine, xt, xfar, xnear, xf_s, xf_r, xn_s, xn_r, x_to, add_part)

    for way in range(2):
        for h in range(2):
            recv(ynear.at[way, h], yn_s.at[way, h], yn_r.at[way, h])
    for h in range(2):
        @pl.loop(0, 8)
        def _(i):
            cols = pl.ds(pl.multiple_of(i * 512, 512), 512)
            total = term[y, h, :, :, cols].astype(F32)
            for way in range(2):
                total += ynear[way, h, :, :, cols].astype(F32)
            term[y, h, :, :, cols] = total.astype(BF)

    for j in range(1, 4):
        zt = lax.rem(zl + j, 4)
        send(
            term.at[y, lax.div(zt, 2), lax.rem(zt, 2)], zrecv.at[j - 1], zr_s.at[j - 1], zr_r.at[j - 1],
            (zt, y, zh, x, c),
        )

    for way in range(2):
        for h in range(2):
            recv(xnear.at[way, h], xn_s.at[way, h], xn_r.at[way, h])
    for h in range(2):
        @pl.loop(0, 16)
        def _(r):
            total = mine[x, h, r].astype(F32)
            for way in range(2):
                total += xnear[way, h, r].astype(F32)
            total = total.astype(BF)
            for col in range(CPD):
                fsum[(h * 16 + r) * CPD + col] = total[col]

    def pick_grads(dz, dy):
        zz = lax.rem(z + dz, 8)
        owner, high = lax.rem(zz, 4) * 4 + lax.rem(y + dy, 4), lax.div(zz, 4)

        @pl.loop(0, RANKS)
        def _(k):
            tile = gpick_ref[owner * RANKS + k]
            gout[high, owner * RANKS + k] = fsum[tile, high]

        return owner, high

    for dz in (4, 3, 5, 2, 6, 1, 7, 0):
        for dy in (2, 1, 3, 0):
            if dz == 0 and dy == 0:
                continue
            owner, high = pick_grads(dz, dy)
            n = dz * 4 + dy
            send(
                gout.at[high, pl.ds(owner * RANKS, RANKS)], garr.at[zh, mine_rows],
                g_s.at[n], g_r.at[n], dev(dz, dy),
            )

    @pl.loop(0, RANKS)
    def _(k):
        garr[zh, me * RANKS + k] = fsum[gpick_ref[me * RANKS + k], zh]

    for j in range(1, 4):
        recv(zrecv.at[j - 1], zr_s.at[j - 1], zr_r.at[j - 1])

    @pl.loop(0, 8)
    def _(i):
        cols = pl.ds(pl.multiple_of(i * 512, 512), 512)
        total = term[y, lax.div(zl, 2), lax.rem(zl, 2), :, cols].astype(F32)
        for j in range(3):
            total += zrecv[j, :, cols].astype(F32)
        dnout[:, cols] = total.astype(BF)

    store_dn = pltpu.make_async_copy(dnout, dn_hbm, ld.at[4])
    store_dn.start()

    for dz in range(8):
        for dy in range(4):
            if dz == 0 and dy == 0:
                continue
            zz = lax.rem(z + 8 - dz, 8)
            source, high = lax.rem(zz, 4) * 4 + lax.rem(y + 4 - dy, 4), lax.div(zz, 4)
            n = dz * 4 + dy
            recv(garr.at[high, pl.ds(source * RANKS, RANKS)], g_s.at[n], g_r.at[n])

    @pl.loop(0, OWN, unroll=4)
    def _(s):
        src = ginv_ref[s]
        total = garr[0, src].astype(F32) + garr[1, src].astype(F32)
        low, high = total[:8], total[8:]
        gres[c, s] = jnp.where(c == 0, low, high)
        give[s] = jnp.where(c == 0, high, low)

    swap = rcopy(give, gres.at[c], q_s.at[0], q_r.at[0], dev(dc=1))
    swap.start()
    sends.append(swap)
    store_a = pltpu.make_async_copy(gres.at[c], gt_hbm.at[c], ld.at[5])
    store_a.start()
    recv(gres.at[other], q_s.at[0], q_r.at[0])
    store_b = pltpu.make_async_copy(gres.at[other], gt_hbm.at[other], ld.at[6])
    store_b.start()
    for copy in sends:
        copy.wait_send()
    for copy in (store_hid, store_dn, store_a, store_b):
        copy.wait()


def step(normed, cotangent, weight_tiles, slot_tile):
    me = lax.axis_index(("zl", "y"))
    lists = index_lists(slot_tile, me)
    dma = pltpu.SemaphoreType.DMA
    scratch = [
        pltpu.VMEM((2, OWN, 16, TILE), BF),
        pltpu.VMEM((160, 2, 16, TILE), BF),
        pltpu.VMEM((160, 2, 16, TILE), BF),
        pltpu.VMEM((4, 4, TOK, D), BF),
        pltpu.VMEM((2, 32, 8, 16, GROUP), BF),
        pltpu.VMEM((GROUP, GROUP), BF),
        pltpu.VMEM((GROUP, GROUP), BF),
        pltpu.VMEM((2, GROUP, GROUP), F32),
        pltpu.VMEM((GROUP, 2 * GROUP), BF),
        pltpu.VMEM((4, 2, 2, TOK, D), BF),
        pltpu.VMEM((2, 2, TOK, D), BF),
        pltpu.VMEM((2, 2, 2, TOK, D), BF),
        pltpu.VMEM((3, TOK, D), BF),
        pltpu.VMEM((TOK, D), BF),
        pltpu.VMEM((2, 4, 2, 16, 4, 2, 16, TILE), BF),
        pltpu.VMEM((4, 2, 16, 4, 2, 16, TILE), BF),
        pltpu.VMEM((2, 16, 4, 2, 16, TILE), BF),
        pltpu.VMEM((2, 2, 16, 4, 2, 16, TILE), BF),
        pltpu.VMEM((OWN, 2, 16, TILE), BF),
        pltpu.VMEM((2, 160, 16, TILE), BF),
        pltpu.VMEM((2, 160, 16, TILE), BF),
        pltpu.VMEM((OWN, 8, TILE), F32),
        pltpu.VMEM((2, OWN, 8, TILE), F32),
        dma((7,)),
    ]
    for shape in (
        (20,), (3,), (4, 2), (4, 2), (2, 2), (2,), (8,), (4,), (2,), (2, 2), (2,), (2, 2), (3,), (32,), (1,),
    ):
        scratch += [dma(shape), dma(shape)]
    smem, anywhere = pl.BlockSpec(memory_space=pltpu.SMEM), pl.BlockSpec(memory_space=pl.ANY)
    return pl.pallas_call(
        kernel,
        out_shape=(
            jax.ShapeDtypeStruct((GROUP, GROUP), BF),
            jax.ShapeDtypeStruct((TOK, D), BF),
            jax.ShapeDtypeStruct((2, OWN, 8, TILE), F32),
        ),
        in_specs=[smem] * 4 + [anywhere] * 3,
        out_specs=[anywhere] * 3,
        scratch_shapes=scratch,
        compiler_params=pltpu.CompilerParams(
            collective_id=0, has_side_effects=True, vmem_limit_bytes=67_043_328
        ),
        name="gated_pair",
    )(*lists, normed, cotangent, weight_tiles)


def solution(mesh):
    finer = Mesh(mesh.devices.reshape(4, 4, 2, 4, 2), AXES)
    tp, dp = ("zl", "y"), ("zh", "x", "c")
    return jax.shard_map(
        step,
        mesh=finer,
        in_specs=(P(dp + tp, None), P(dp, tp), P(None, tp, None, None), P()),
        out_specs=(P(dp, tp), P(dp + tp, None), P(None, tp, dp, None)),
        check_vma=False,
    )
```

time: 498 us -> 193 us (0.39); the launches traced: 491 us -> 193 us
  waiting for transfers between devices: 340 us -> 0 us
  Pallas kernels: 0 us -> 180 us
  local copies, waits for them, and re-layouts: 88.3 us -> 6.55 us
  matrix products: 28.3 us -> 0 us
  between operations: 14.4 us -> 0.69 us
  starting transfers between devices: 9.98 us -> 0 us
    pallas_call x0 -> x1, Pallas kernels: none -> 180 us  [step(): pl.pallas_call(kernel, out_shape=(jax.ShapeDtypeStruct((GROUP, GROUP), BF...]
    all_gather x3 -> x0, waiting for transfers between devices: 163 us -> none  [the longest x1 111 us: local(): weight_block = lax.all_gather(partial_tiles, 'dp', axis=2, tiled=True)]
    unnamed x7 -> x0, waiting for transfers between devices: 140 us -> none
    unnamed x17 -> x5, local copies, waits for them, and re-layouts: 40.9 us -> 5.8 us
    all_to_all x2 -> x0, waiting for transfers between devices: 31.2 us -> none  [the longest x1 18.1 us: local(): lax.all_to_all(outgoing_grads.astype(jnp.bfloat16), TP, split_axis=1, con...]
    dot_general x3 -> x0, matrix products: 28.3 us -> none  [the longest x1 10.6 us: local(): jnp.einsum('nri,mrcij->nmcj', tiled_in, weight_block, preferred_element_t...]
    scatter x2 -> x0, local copies, waits for them, and re-layouts: 13.7 us -> none  [place_tiles(): return empty.at[:, places.reshape(-1)].set(flat, mode='drop')]
    convert_element_type x1 -> x0, local copies, waits for them, and re-layouts: 12 us -> none  [local(): partial_value = jnp.einsum('nri,nmcj->mrcij', tiled_in, grads_in, preferr...]
  transfers between devices with their start and end apart: 8 -> 0, of which waited for: 7 -> 0; matrix products, arithmetic and copies ran while one was open for 19% -> 0% of each run, Pallas kernels for 0% -> 0%
where the time goes in v1:
time: 193 us
  Pallas kernels  180 us (93%)
  local copies, waits for them, and re-layouts  6.55 us (3%)
  other arithmetic  6.02 us (3%)
    pallas_call x1, Pallas kernels, step(): pl.pallas_call(kernel, out_shape=(jax.ShapeDtypeStruct((GROUP, GROUP), BF...  180 us
    unnamed x5, local copies, waits for them, and re-layouts  5.8 us

profile of v1, /device:TPU:1, one launch (start us, length us, event | category | flops | bytes accessed | tf_op | source)
XLA Modules:
  0.0 192.8 jit_solution(3761586072013970518)
XLA Ops:
  0.6 0.7 broadcast_compare_fusion
  1.4 0.7 fusion.5
  2.1 0.6 convert_reduce_fusion
  2.8 0.0 copy-start
  2.8 0.7 select_reduce_fusion.2.pick_ref
  3.5 0.1 broadcast_add_fusion
  3.5 2.9 %select_reduce_fusion.inv_ref = s32[128]{0:T(128)} fusion(s32[16,128]{1,0:T(8,128)S(1)} %broadcast_add_fusion, s32[16,128]{1,0:T(8,128)S(1)} %get-tuple-element.3, pred[16,128]{1,0:T(8,128)(4,1)S(1)} %broadcast_compare_fusion), kind=kLoop, calls=%fused_computation | loop fusion | flops 1048448 | bytes 18944 | tf_op jit(solution)/shard_map/reduce_sum | solution.py:43
  6.5 0.0 copy-done
  6.5 0.2 select_reduce_fusion.1
  6.7 0.1 copy.7
  6.8 0.7 reshape.243.gpick_ref
  7.4 179.5 %gated_pair.1 = (bf16[512,512]{1,0:T(8,128)(2,1)}, bf16[32,4096]{1,0:T(8,128)(2,1)}, f32[2,128,8,128]{3,2,1,0:T(8,128)}) custom-call(s32[160]{0:T(256)} %select_reduce_fusion.2.pick_ref, s32[128]{0:T(128)} %select_reduce_fusion.inv_ref, s32[160]{0:T(256)} %reshape.243.gpick_ref, s32[128]{0:T(128)} %copy-done, bf16[32,4096]{1,0:T(8,128)(2,1)} %tok_hbm.1, ...), custom_call_target="tpu_custom_call" | custom-call | tf_op jit(solution)/shard_map/gated_pair/pallas_call | solution.py:488
  187.0 1.9 copy.11
  188.9 1.7 copy.12
  190.5 2.3 %copy.13 = f32[2,128,8,128]{3,2,1,0:T(8,128)} copy(f32[2,128,8,128]{3,2,1,0:T(8,128)} %get-tuple-element.10) | data formatting | bytes 2097152
  (3 shorter events, 0.0 us)
Async XLA Ops:
  2.8 3.7 %copy-start = (s32[128]{0:T(128)}, s32[128]{0:T(128)S(1)}, u32[]{:S(2)}) copy-start(s32[128]{0:T(128)S(1)} %add_bitcast_fusion.ginv_ref) | copy-start | bytes 1540

commit v2 on v1

v2 whole, which is shorter than its diff:
```python
import jax
import jax.numpy as jnp
from jax import lax
from jax.experimental import pallas as pl
from jax.experimental.pallas import tpu as pltpu
from jax.sharding import Mesh
from jax.sharding import PartitionSpec as P

D = 4096
FW = 8192
TILE = 128
TC = FW // TILE
OWNERS = 16
OWN = 128
CPD = TC // OWNERS
RANKS = 10
TOK = 32
GROUP = 512
AXES = ("zl", "y", "zh", "x", "c")
MESH = pl.DeviceIdType.MESH
BF = jnp.bfloat16
F32 = jnp.float32
SENT = tuple(
    [(m, dz, dy) for m in range(2) for dz in (2, 6, 1, 7, 0) for dy in range(4)
     if (dz or dy) and (dz not in (2, 6) or (dz == 2) == ((dy < 2) == (m == 0)))]
)
STAGES = 4
COLS = D // STAGES


def kernel(
    tiles_ref, tok_hbm, cot_hbm, own_hbm,
    hid_hbm, dn_hbm, gt_hbm,
    keys, rows, lists, own, outg, arrv_a, arrv_b, xs, ws, cot, hid, acc, grads, term, yfar, ynear, zrecv, dnout,
    part, precv, xfar, xnear, fsum, gout, garr, give, gres,
    ld, a_s, a_r, tz_s, tz_r, tn_s, tn_r, tf_s, tf_r, wn_s, wn_r, wf_s, wf_r, wd_s, wd_r,
    pd_s, pd_r, xf_s, xf_r, xn_s, xn_r, yf_s, yf_r, yn_s, yn_r, zr_s, zr_r, g_s, g_r, q_s, q_r,
):
    zl, y, zh, x, c = (lax.axis_index(a) for a in AXES)
    z = zh * 4 + zl
    me = zl * 4 + y
    other = 1 - c

    def dev(dz=0, dy=0, dx=0, dc=0):
        zz = lax.rem(z + dz, 8)
        return (
            lax.rem(zz, 4), lax.rem(y + dy, 4), lax.div(zz, 4), lax.rem(x + dx, 4), lax.rem(c + dc, 2),
        )

    def rcopy(src, dst, ss, rs, to):
        return pltpu.make_async_remote_copy(
            src_ref=src, dst_ref=dst, send_sem=ss, recv_sem=rs, device_id=to, device_id_type=MESH
        )

    arrv = (arrv_a, arrv_b)
    scopes = []

    def phase(name):
        if scopes:
            scopes.pop().__exit__(None, None, None)
        if name:
            scopes.append(jax.named_scope(name))
            scopes[-1].__enter__()

    sends = []

    def send(src, dst, ss, rs, to):
        copy = rcopy(src, dst, ss, rs, to)
        copy.start()
        sends.append(copy)

    def recv(dst, ss, rs):
        rcopy(dst, dst, ss, rs, dev(dc=1)).wait_recv()

    phase("p00_load")
    band = x * 2 + c
    load_own = pltpu.make_async_copy(
        own_hbm.at[:, :, pl.ds(pl.multiple_of(band * 16, 16), 16), :], own, ld.at[0]
    )
    load_tok = pltpu.make_async_copy(tok_hbm, xs.at[zl, y], ld.at[1])
    load_cot = pltpu.make_async_copy(cot_hbm, cot, ld.at[2])
    load_tok.start()
    load_own.start()

    barrier = pltpu.get_barrier_semaphore()

    @pl.loop(1, 32)
    def _(j):
        dz, dy = lax.div(j, 4), lax.rem(j, 4)
        pl.semaphore_signal(barrier, inc=1, device_id=dev(dz, dy), device_id_type=MESH)

    for to in (dev(dx=1), dev(dx=3), dev(dc=1)):
        pl.semaphore_signal(barrier, inc=1, device_id=to, device_id_type=MESH)

    phase("p01_lists")
    tiles = tiles_ref[...]
    lane = lax.broadcasted_iota(jnp.int32, (OWNERS, OWN), 1)
    owner_id = lax.broadcasted_iota(jnp.int32, (OWNERS, OWN), 0)
    target = lax.shift_right_logical(tiles & (TC - 1), 2)
    place = lax.shift_right_logical(tiles, 6) * CPD + (tiles & (TC - 1)) - me * CPD
    rank = jnp.zeros_like(tiles)
    for t in range(OWNERS):
        hit = target == t
        count = jnp.where(hit, 1, 0)
        for step_of in (1, 2, 4, 8, 16, 32, 64):
            count += jnp.where(lane >= step_of, pltpu.roll(count, step_of, 1), 0)
        rank = jnp.where(hit, count - 1, rank)
    mine = target == me
    last = OWNERS * RANKS - 1
    source = jnp.minimum(owner_id * RANKS + rank, last)
    code = jnp.minimum(target * RANKS + rank, last)
    my_code = jnp.max(jnp.where(owner_id == me, code, 0), axis=0, keepdims=True)
    keys[0:16] = jnp.where(mine, place, -1)
    keys[16:32] = source
    keys[32:48] = jnp.where(mine, source, -1)
    keys[48:64] = place
    keys[64:128] = jnp.broadcast_to(my_code, (64, OWN))
    keys[...] = keys[...].T
    wide = lax.broadcasted_iota(jnp.int32, (8, 2 * OWN), 1)
    seq = lax.broadcasted_iota(jnp.int32, (8, 2 * OWN), 0)

    def fold(i, sums):
        col = keys[pl.ds(pl.multiple_of(i * 8, 8), 8)]
        inverse, gpick, pick = sums
        for o in range(OWNERS):
            hit_a = jnp.where(col[:, o : o + 1] == wide, col[:, 16 + o : 17 + o], 0)
            hit_b = jnp.where(col[:, 32 + o : 33 + o] == wide, col[:, 48 + o : 49 + o], 0)
            inverse, gpick = jnp.maximum(inverse, hit_a), jnp.maximum(gpick, hit_b)
        pick = jnp.maximum(pick, jnp.where(col[:, 64:65] == wide, seq + i * 8, 0))
        return inverse, gpick, pick

    zero = jnp.zeros((8, 2 * OWN), jnp.int32)
    inverse, gpick, pick = lax.fori_loop(0, 16, fold, (zero, zero, zero))
    rows[0:1] = jnp.max(pick, axis=0, keepdims=True)
    rows[1:2] = jnp.max(inverse, axis=0, keepdims=True)
    rows[2:3] = jnp.max(gpick, axis=0, keepdims=True)
    rows[3:4, :OWN] = my_code
    rows[3:4, OWN:] = my_code
    load_lists = pltpu.make_async_copy(rows, lists, ld.at[7])
    load_lists.start()

    phase("p02_barrier")
    pl.semaphore_wait(barrier, 34)
    load_cot.start()
    load_tok.wait()

    def zq_of(q):
        return lax.rem(zl + 4 - q, 4)

    def near_tokens(q):
        block = xs.at[zq_of(q), y]
        for way, dy in ((0, 1), (1, 3)):
            send(block, block, tn_s.at[q, way], tn_r.at[q, way], dev(dy=dy))

    def far_tokens(q):
        for way, dy in ((0, 1), (1, 3)):
            src = lax.rem(y + 4 - dy, 4)
            recv(xs.at[zq_of(q), src], tn_s.at[q, way], tn_r.at[q, way])
            half = xs.at[zq_of(q), src, pl.ds(16 * way, 16)]
            send(half, half, tf_s.at[q, way], tf_r.at[q, way], dev(dy=dy))

    def last_tokens(q):
        src = lax.rem(y + 2, 4)
        for way in range(2):
            recv(xs.at[zq_of(q), src, pl.ds(16 * way, 16)], tf_s.at[q, way], tf_r.at[q, way])

    near_tokens(0)

    phase("p03_pick_send")
    load_lists.wait()
    load_own.wait()
    my_rows = pl.ds(me * RANKS, RANKS)

    def tp_of(dz, dy):
        return lax.rem(lax.rem(z + dz, 8), 4) * 4 + lax.rem(y + dy, 4)

    def pick_into(dst, m, t):
        @pl.loop(0, RANKS)
        def _(k):
            dst[t * RANKS + k] = own[m, lists[0, t * RANKS + k]]

    for n, (m, dz, dy) in enumerate(SENT):
        t = tp_of(dz, dy)
        pick_into(outg.at[m], m, t)
        send(outg.at[m, pl.ds(t * RANKS, RANKS)], arrv[m].at[my_rows], a_s.at[n], a_r.at[n], dev(dz, dy))
    for m in range(2):
        pick_into(arrv[m], m, me)

    phase("p04_tokz")
    for j in (1, 3, 2):
        to = (lax.rem(zl + j, 4), y, zh, x, c)
        send(xs.at[zl, y], xs.at[zl, y], tz_s.at[j - 1], tz_r.at[j - 1], to)

    def side_band(way, core):
        return lax.rem(x + (3 if way == 0 else 1), 4) * 2 + core

    far_x = lax.rem(x + 2, 4) * 2
    x_to = (dev(dx=1), dev(dx=3))
    y_to = (dev(dy=1), dev(dy=3))

    def own_weights(m):
        phase(f"p05_wait_a2a{m}")
        for n, (mm, dz, dy) in enumerate(SENT):
            if mm == m:
                t = tp_of(8 - dz, 4 - dy)
                recv(arrv[m].at[pl.ds(t * RANKS, RANKS)], a_s.at[n], a_r.at[n])
        phase(f"p06_place{m}")

        @pl.loop(0, D // TILE)
        def _(r):
            for col in range(CPD):
                ws[m, r, band, :, col * TILE : (col + 1) * TILE] = arrv[m][lists[1, r * CPD + col]]

        block = ws.at[m, :, band]
        for way in range(2):
            send(block, block, wn_s.at[m, way], wn_r.at[m, way], x_to[way])
        send(block, block, wd_s.at[m, 0], wd_r.at[m, 0], dev(dc=1))

    def near_weights(m):
        phase(f"p09_nearw{m}")
        for way in range(2):
            block = ws.at[m, :, side_band(way, c)]
            recv(block, wn_s.at[m, way], wn_r.at[m, way])
            half = ws.at[m, pl.ds(16 * way, 16), side_band(way, c)]
            send(half, half, wf_s.at[m, way], wf_r.at[m, way], x_to[way])
            send(block, block, wd_s.at[m, 1 + way], wd_r.at[m, 1 + way], dev(dc=1))

    def far_weights(m):
        phase(f"p13_farw{m}")
        for way in range(2):
            half = ws.at[m, pl.ds(16 * way, 16), far_x + c]
            recv(half, wf_s.at[m, way], wf_r.at[m, way])
            send(half, half, wd_s.at[m, 3 + way], wd_r.at[m, 3 + way], dev(dc=1))

    def partner_weights(m):
        phase(f"p15_d2d{m}")
        recv(ws.at[m, :, x * 2 + other], wd_s.at[m, 0], wd_r.at[m, 0])
        for way in range(2):
            recv(ws.at[m, :, side_band(way, other)], wd_s.at[m, 1 + way], wd_r.at[m, 1 + way])
            recv(ws.at[m, pl.ds(16 * way, 16), far_x + other], wd_s.at[m, 3 + way], wd_r.at[m, 3 + way])

    def tokens_z(q):
        phase(f"p07_tokz{q}")
        recv(xs.at[zq_of(q), y], tz_s.at[q - 1], tz_r.at[q - 1])
        near_tokens(q)

    own_weights(0)
    own_weights(1)
    phase("p08_far0")
    far_tokens(0)
    tokens_z(1)
    tokens_z(3)
    near_weights(0)
    tokens_z(2)
    phase("p10_far1")
    far_tokens(1)
    near_weights(1)
    phase("p10_far3")
    far_tokens(3)
    far_weights(0)
    phase("p10_far2")
    far_tokens(2)
    far_weights(1)
    partner_weights(0)
    partner_weights(1)
    phase("p14_lasttok")
    for q in (0, 1, 3, 2):
        last_tokens(q)

    phase("p16_fwd")

    @pl.loop(0, 4)
    def _(k):
        cols = pl.ds(pl.multiple_of(k * 1024, 1024), 1024)
        a = xs[:, :, :, cols].reshape(GROUP, 1024)
        for m in range(2):
            w = ws[m, pl.ds(k * 8, 8)].reshape(1024, GROUP)
            v = jnp.dot(a, w, preferred_element_type=F32)

            @pl.when(k == 0)
            def _():
                acc[m] = v

            @pl.when(k > 0)
            def _():
                acc[m] += v

    phase("p17_elem")
    load_cot.wait()

    @pl.loop(0, 16)
    def _(i):
        rows_of = pl.ds(pl.multiple_of(i * 32, 32), 32)
        gate, up = acc[0, rows_of], acc[1, rows_of]
        s = jax.nn.sigmoid(gate)
        act = gate * s
        ct = cot[rows_of].astype(F32)
        hid[rows_of] = (act * up).astype(BF)
        grads[rows_of, :GROUP] = (ct * up * (s * (1.0 + gate * (1.0 - s)))).astype(BF)
        grads[rows_of, GROUP:] = (ct * act).astype(BF)

    store_hid = pltpu.make_async_copy(hid, hid_hbm, ld.at[3])
    store_hid.start()

    def share(st):
        phase(f"p20_dn{st}")

        @pl.loop(0, COLS // 512)
        def _(d):
            v = None
            for m in range(2):
                w = ws[m, pl.ds(st * (COLS // TILE) + d * 4, 4)].reshape(GROUP, GROUP)
                g = grads[:, m * GROUP : (m + 1) * GROUP]
                t = lax.dot_general(g, w, (((1,), (1,)), ((), ())), preferred_element_type=F32)
                v = t if v is None else v + t
            v = v.astype(BF).reshape(2, 2, 4, TOK, 512)
            cols = pl.ds(pl.multiple_of(d * 512, 512), 512)
            for yy in range(4):
                term[st, yy, :, :, :, cols] = v[:, :, yy]

    def ring(pos):
        return lax.rem(pos + 2, 4), lax.rem(pos + 1, 4), lax.rem(pos + 3, 4), pos

    xt, yt = ring(x), ring(y)

    def ring_open(a, t, far, near, fs, fr, ss, rs, to):
        for way in range(2):
            send(a(t[0], way), far.at[way], fs.at[way], fr.at[way], to[way])
        for way in range(2):
            h = 1 - way
            send(a(t[1 + way], h), near.at[way, h], ss.at[way, h], rs.at[way, h], to[way])

    def ring_pass(a, t, far, near, fs, fr, ss, rs, to, add):
        for way in range(2):
            recv(far.at[way], fs.at[way], fr.at[way])
            add(t[1 + way], way)
            send(a(t[1 + way], way), near.at[way, way], ss.at[way, way], rs.at[way, way], to[way])

    def ring_close(near, ss, rs):
        for way in range(2):
            for h in range(2):
                recv(near.at[way, h], ss.at[way, h], rs.at[way, h])

    def y_args(st):
        a = lambda t, h: term.at[st, t, h]
        return a, yt, yfar.at[st], ynear.at[st], yf_s.at[st], yf_r.at[st], yn_s.at[st], yn_r.at[st], y_to

    def y_open(st):
        ring_open(*y_args(st))

    def y_pass(st):
        phase(f"p23_ypass{st}")

        def add(t, way):
            here = term[st, t, way].astype(F32)
            term[st, t, way] = (here + yfar[st, way].astype(F32)).astype(BF)

        ring_pass(*y_args(st), add)

    def y_close(st):
        phase(f"p25_yclose{st}")
        ring_close(ynear.at[st], yn_s.at[st], yn_r.at[st])
        for h in range(2):
            total = term[st, y, h].astype(F32)
            for way in range(2):
                total += ynear[st, way, h].astype(F32)
            term[st, y, h] = total.astype(BF)
        for j in range(1, 4):
            zt = lax.rem(zl + j, 4)
            send(
                term.at[st, y, lax.div(zt, 2), lax.rem(zt, 2)], zrecv.at[st, j - 1],
                zr_s.at[st, j - 1], zr_r.at[st, j - 1], (zt, y, zh, x, c),
            )

    highs = (1 - zh, zh)
    mat = part.at[c]

    def partner_sum(k):
        phase(f"p22_partner{k}")
        for i in range(4):
            recv(precv.at[xt[i], highs[k]], pd_s.at[k, i], pd_r.at[k, i])
            for h in range(2):

                @pl.loop(0, 4)
                def _(r):
                    at = (xt[i], highs[k], h, pl.ds(r * 4, 4))
                    mat[at] = (mat[at].astype(F32) + precv[at].astype(F32)).astype(BF)

    def x_args(k):
        a = lambda t, h: mat.at[t, highs[k], h]
        return a, xt, xfar.at[k], xnear.at[k], xf_s.at[k], xf_r.at[k], xn_s.at[k], xn_r.at[k], x_to

    def x_open(k):
        ring_open(*x_args(k))

    def x_pass(k):
        phase(f"p24_xpass{k}")

        def add(t, way):
            @pl.loop(0, 4)
            def _(r):
                rs = pl.ds(r * 4, 4)
                at = (t, highs[k], way, rs)
                mat[at] = (mat[at].astype(F32) + xfar[k, way, rs].astype(F32)).astype(BF)

        ring_pass(*x_args(k), add)

    def x_close(k):
        phase(f"p27_xclose{k}")
        ring_close(xnear.at[k], xn_s.at[k], xn_r.at[k])
        for h in range(2):

            @pl.loop(0, 16)
            def _(r):
                total = mat[x, highs[k], h, r].astype(F32)
                for way in range(2):
                    total += xnear[k, way, h, r].astype(F32)
                fsum[k, pl.ds((h * 16 + r) * CPD, CPD)] = total.astype(BF)

        for dzl in (0, 1, 3, 2):
            for dy in (2, 1, 3, 0):
                owner = lax.rem(zl + dzl, 4) * 4 + lax.rem(y + dy, 4)
                here = k == 1 and dzl == 0 and dy == 0

                @pl.loop(0, RANKS)
                def _(i):
                    tile = fsum[k, lists[2, owner * RANKS + i]]
                    if here:
                        garr[zh, owner * RANKS + i] = tile
                    else:
                        gout[k, owner * RANKS + i] = tile

                if not here:
                    n = dzl * 4 + dy
                    to = (lax.rem(zl + dzl, 4), lax.rem(y + dy, 4), highs[k], x, c)
                    send(
                        gout.at[k, pl.ds(owner * RANKS, RANKS)], garr.at[zh, my_rows],
                        g_s.at[k, n], g_r.at[k, n], to,
                    )

    share(0)
    y_open(0)

    phase("p18_dw")

    @pl.loop(0, 8)
    def _(d):
        cols = pl.ds(pl.multiple_of(d * 512, 512), 512)
        a = xs[:, :, :, cols].reshape(GROUP, 512)
        v = lax.dot_general(a, grads[...], (((0,), (0,)), ((), ())), preferred_element_type=F32)
        v = v.astype(BF).reshape(4, 2, 4, 16, 1024)
        half, row = lax.div(d, 4), lax.rem(d, 4) * 4
        for m in range(2):
            for xx in range(4):
                for col in range(CPD):
                    lo = m * GROUP + col * TILE
                    for high in range(2):
                        part[m, xx, high, half, pl.ds(row, 4), col] = v[:, high, xx, :, lo : lo + TILE]

    for k in range(2):
        for i in range(4):
            send(
                part.at[other, xt[i], highs[k]], precv.at[xt[i], highs[k]],
                pd_s.at[k, i], pd_r.at[k, i], dev(dc=1),
            )

    y_pass(0)
    share(1)
    y_open(1)
    partner_sum(0)
    x_open(0)
    share(2)
    share(3)
    partner_sum(1)
    y_pass(1)
    y_open(2)
    y_close(0)
    x_pass(0)
    x_open(1)
    y_close(1)
    y_pass(2)
    y_open(3)
    y_close(2)
    x_close(0)
    y_pass(3)
    x_pass(1)
    y_close(3)
    x_close(1)

    phase("p30_zrecv")
    for st in range(STAGES):
        for j in range(1, 4):
            recv(zrecv.at[st, j - 1], zr_s.at[st, j - 1], zr_r.at[st, j - 1])
        total = term[st, y, lax.div(zl, 2), lax.rem(zl, 2)].astype(F32)
        for j in range(3):
            total += zrecv[st, j].astype(F32)
        dnout[:, st * COLS : (st + 1) * COLS] = total.astype(BF)

    store_dn = pltpu.make_async_copy(dnout, dn_hbm, ld.at[4])
    store_dn.start()

    for k in range(2):
        phase(f"p31_ga2a{k}")
        for n in range(16):
            if k == 1 and n == 0:
                continue
            dzl, dy = divmod(n, 4)
            src = lax.rem(zl + 4 - dzl, 4) * 4 + lax.rem(y + 4 - dy, 4)
            recv(garr.at[highs[k], pl.ds(src * RANKS, RANKS)], g_s.at[k, n], g_r.at[k, n])

    phase("p32_final")

    @pl.loop(0, OWN, unroll=4)
    def _(s):
        src = lists[3, s]
        total = garr[0, src].astype(F32) + garr[1, src].astype(F32)
        low, high = total[:8], total[8:]
        gres[c, s] = jnp.where(c == 0, low, high)
        give[s] = jnp.where(c == 0, high, low)

    phase("p33_swap")
    send(give, gres.at[c], q_s.at[0], q_r.at[0], dev(dc=1))
    store_a = pltpu.make_async_copy(gres.at[c], gt_hbm.at[c], ld.at[5])
    store_a.start()
    recv(gres.at[other], q_s.at[0], q_r.at[0])
    store_b = pltpu.make_async_copy(gres.at[other], gt_hbm.at[other], ld.at[6])
    store_b.start()
    phase("p34_drain")
    for copy in sends:
        copy.wait_send()
    for copy in (store_hid, store_dn, store_a, store_b):
        copy.wait()
    phase(None)


def step(normed, cotangent, weight_tiles, slot_tile):
    dma = pltpu.SemaphoreType.DMA
    scratch = [
        pltpu.VMEM((OWN, OWN), jnp.int32),
        pltpu.VMEM((8, 2 * OWN), jnp.int32),
        pltpu.SMEM((8, 2 * OWN), jnp.int32),
        pltpu.VMEM((2, OWN, 16, TILE), BF),
        pltpu.VMEM((2, 160, 16, TILE), BF),
        pltpu.VMEM((160, 16, TILE), BF),
        pltpu.VMEM((160, 16, TILE), BF),
        pltpu.VMEM((4, 4, TOK, D), BF),
        pltpu.VMEM((2, 32, 8, 16, GROUP), BF),
        pltpu.VMEM((GROUP, GROUP), BF),
        pltpu.VMEM((GROUP, GROUP), BF),
        pltpu.VMEM((2, GROUP, GROUP), F32),
        pltpu.VMEM((GROUP, 2 * GROUP), BF),
        pltpu.VMEM((STAGES, 4, 2, 2, TOK, COLS), BF),
        pltpu.VMEM((STAGES, 2, 2, TOK, COLS), BF),
        pltpu.VMEM((STAGES, 2, 2, 2, TOK, COLS), BF),
        pltpu.VMEM((STAGES, 3, TOK, COLS), BF),
        pltpu.VMEM((TOK, D), BF),
        pltpu.VMEM((2, 4, 2, 2, 16, 4, 16, TILE), BF),
        pltpu.VMEM((4, 2, 2, 16, 4, 16, TILE), BF),
        pltpu.VMEM((2, 2, 16, 4, 16, TILE), BF),
        pltpu.VMEM((2, 2, 2, 16, 4, 16, TILE), BF),
        pltpu.VMEM((2, OWN, 16, TILE), BF),
        pltpu.VMEM((2, 160, 16, TILE), BF),
        pltpu.VMEM((2, 160, 16, TILE), BF),
        pltpu.VMEM((OWN, 8, TILE), F32),
        pltpu.VMEM((2, OWN, 8, TILE), F32),
        dma((8,)),
    ]
    for shape in (
        (len(SENT),), (3,), (4, 2), (4, 2), (2, 2), (2, 2), (2, 5), (2, 4), (2, 2), (2, 2, 2),
        (STAGES, 2), (STAGES, 2, 2), (STAGES, 3), (2, 16), (1,),
    ):
        scratch += [dma(shape), dma(shape)]
    anywhere = pl.BlockSpec(memory_space=pl.ANY)
    return pl.pallas_call(
        kernel,
        out_shape=(
            jax.ShapeDtypeStruct((GROUP, GROUP), BF),
            jax.ShapeDtypeStruct((TOK, D), BF),
            jax.ShapeDtypeStruct((2, OWN, 8, TILE), F32),
        ),
        in_specs=[pl.BlockSpec(memory_space=pltpu.VMEM)] + [anywhere] * 3,
        out_specs=[anywhere] * 3,
        scratch_shapes=scratch,
        compiler_params=pltpu.CompilerParams(
            collective_id=0, has_side_effects=True, vmem_limit_bytes=67_043_328
        ),
        name="gated_pair",
    )(slot_tile.reshape(OWNERS, OWN), normed, cotangent, weight_tiles)


def solution(mesh):
    finer = Mesh(mesh.devices.reshape(4, 4, 2, 4, 2), AXES)
    tp, dp = ("zl", "y"), ("zh", "x", "c")
    return jax.shard_map(
        step,
        mesh=finer,
        in_specs=(P(dp + tp, None), P(dp, tp), P(None, tp, None, None), P()),
        out_specs=(P(dp, tp), P(dp + tp, None), P(None, tp, dp, None)),
        check_vma=False,
    )
```

time: 193 us -> 161 us (0.83)
  Pallas kernels: 180 us -> 154 us
  other arithmetic: 6.02 us -> 0 us
    pallas_call x1, Pallas kernels: 180 us -> 154 us  [step(): pl.pallas_call(kernel, out_shape=(jax.ShapeDtypeStruct((GROUP, GROUP), BF...]
    reduce_sum x4 -> x0, other arithmetic: 4.48 us -> none  [the longest x1 2.92 us: index_lists(): jnp.sum(jnp.where(mine[None] & (place[None] == seq[:, None, None]), sourc...]
    unnamed x5 -> x3, local copies, waits for them, and re-layouts: 5.8 us -> 5.8 us
where the time goes in v2:
time: 161 us
  Pallas kernels  154 us (96%)
  local copies, waits for them, and re-layouts  5.8 us (4%)
    pallas_call x1, Pallas kernels, step(): pl.pallas_call(kernel, out_shape=(jax.ShapeDtypeStruct((GROUP, GROUP), BF...  154 us
    unnamed x3, local copies, waits for them, and re-layouts  5.8 us

profile of v2, /device:TPU:1, one launch (start us, length us, event | category | flops | bytes accessed | tf_op | source)
XLA Modules:
  0.0 160.7 jit_solution(12047995291113134356)
XLA Ops:
  0.6 154.3 %gated_pair.1 = (bf16[512,512]{1,0:T(8,128)(2,1)}, bf16[32,4096]{1,0:T(8,128)(2,1)}, f32[2,128,8,128]{3,2,1,0:T(8,128)}) custom-call(s32[16,128]{1,0:T(8,128)} %bitcast.1, bf16[32,4096]{1,0:T(8,128)(2,1)} %tok_hbm.1, bf16[512,512]{1,0:T(8,128)(2,1)} %cot_hbm.1, bf16[2,128,128,128]{3,2,1,0:T(8,128)(2,1)} %own_hbm.1), custom_call_target="tpu_custom_call" | custom-call | tf_op jit(solution)/shard_map/gated_pair/pallas_call | solution.py:574
  154.9 1.9 %copy.10 = bf16[512,512]{1,0:T(8,128)(2,1)} copy(bf16[512,512]{1,0:T(8,128)(2,1)} %get-tuple-element.6) | data formatting | bytes 1048576
  156.8 1.7 %copy.11 = bf16[32,4096]{1,0:T(8,128)(2,1)} copy(bf16[32,4096]{1,0:T(8,128)(2,1)} %get-tuple-element.7) | data formatting | bytes 524288
  158.5 2.3 %copy.12 = f32[2,128,8,128]{3,2,1,0:T(8,128)} copy(f32[2,128,8,128]{3,2,1,0:T(8,128)} %get-tuple-element.8) | data formatting | bytes 2097152

commit v3 on v2

--- a/solution.py
+++ b/solution.py
@@ -31,7 +31,7 @@
 def kernel(
     tiles_ref, tok_hbm, cot_hbm, own_hbm,
     hid_hbm, dn_hbm, gt_hbm,
-    keys, rows, lists, own, outg, arrv_a, arrv_b, xs, ws, cot, hid, acc, grads, term, yfar, ynear, zrecv, dnout,
+    keys, rows, lists, own, outg, arrv_a, arrv_b, xs, ws, cot, hid, acc, grads, term, yfar, ynear, zpair, zcross, dnout,
     part, precv, xfar, xnear, fsum, gout, garr, give, gres,
     ld, a_s, a_r, tz_s, tz_r, tn_s, tn_r, tf_s, tf_r, wn_s, wn_r, wf_s, wf_r, wd_s, wd_r,
     pd_s, pd_r, xf_s, xf_r, xn_s, xn_r, yf_s, yf_r, yn_s, yn_r, zr_s, zr_r, g_s, g_r, q_s, q_r,
@@ -98,105 +98,117 @@
     owner_id = lax.broadcasted_iota(jnp.int32, (OWNERS, OWN), 0)
     target = lax.shift_right_logical(tiles & (TC - 1), 2)
     place = lax.shift_right_logical(tiles, 6) * CPD + (tiles & (TC - 1)) - me * CPD
-    rank = jnp.zeros_like(tiles)
-    for t in range(OWNERS):
-        hit = target == t
-        count = jnp.where(hit, 1, 0)
-        for step_of in (1, 2, 4, 8, 16, 32, 64):
-            count += jnp.where(lane >= step_of, pltpu.roll(count, step_of, 1), 0)
-        rank = jnp.where(hit, count - 1, rank)
+    shift = (target & 7) * 4
+    one = lax.shift_left(jnp.ones_like(tiles), shift)
+    count = [jnp.where(target < 8, one, 0), jnp.where(target < 8, 0, one)]
+    for step_of in (1, 2, 4, 8, 16, 32, 64):
+        count = [v + jnp.where(lane >= step_of, pltpu.roll(v, step_of, 1), 0) for v in count]
+    count = jnp.where(target < 8, count[0], count[1])
+    rank = jnp.maximum((lax.shift_right_logical(count, shift) & 15) - 1, 0)
     mine = target == me
     last = OWNERS * RANKS - 1
     source = jnp.minimum(owner_id * RANKS + rank, last)
     code = jnp.minimum(target * RANKS + rank, last)
     my_code = jnp.max(jnp.where(owner_id == me, code, 0), axis=0, keepdims=True)
-    keys[0:16] = jnp.where(mine, place, -1)
-    keys[16:32] = source
-    keys[32:48] = jnp.where(mine, source, -1)
-    keys[48:64] = place
-    keys[64:128] = jnp.broadcast_to(my_code, (64, OWN))
-    keys[...] = keys[...].T
-    wide = lax.broadcasted_iota(jnp.int32, (8, 2 * OWN), 1)
-    seq = lax.broadcasted_iota(jnp.int32, (8, 2 * OWN), 0)
-
-    def fold(i, sums):
-        col = keys[pl.ds(pl.multiple_of(i * 8, 8), 8)]
-        inverse, gpick, pick = sums
-        for o in range(OWNERS):
-            hit_a = jnp.where(col[:, o : o + 1] == wide, col[:, 16 + o : 17 + o], 0)
-            hit_b = jnp.where(col[:, 32 + o : 33 + o] == wide, col[:, 48 + o : 49 + o], 0)
-            inverse, gpick = jnp.maximum(inverse, hit_a), jnp.maximum(gpick, hit_b)
-        pick = jnp.maximum(pick, jnp.where(col[:, 64:65] == wide, seq + i * 8, 0))
-        return inverse, gpick, pick
-
-    zero = jnp.zeros((8, 2 * OWN), jnp.int32)
-    inverse, gpick, pick = lax.fori_loop(0, 16, fold, (zero, zero, zero))
-    rows[0:1] = jnp.max(pick, axis=0, keepdims=True)
-    rows[1:2] = jnp.max(inverse, axis=0, keepdims=True)
-    rows[2:3] = jnp.max(gpick, axis=0, keepdims=True)
+    key_a, key_b = jnp.where(mine, place, -1), jnp.where(mine, source, -1)
+    codes = lax.broadcasted_iota(jnp.int32, (OWNERS * RANKS, OWN), 0)
+    spot = codes[:OWN]
+    inverse, gpick = jnp.zeros_like(spot), jnp.zeros_like(codes)
+    for o in range(OWNERS):
+        row = slice(o, o + 1)
+        inverse = jnp.maximum(inverse, jnp.where(key_a[row] == spot, source[row], 0))
+        gpick = jnp.maximum(gpick, jnp.where(key_b[row] == codes, place[row], 0))
+    wide = lax.broadcasted_iota(jnp.int32, codes.shape, 1)
+    pick = jnp.max(jnp.where(my_code == codes, wide, 0), axis=1, keepdims=True)
+    inverse = jnp.max(inverse, axis=1, keepdims=True)
+    gpick = jnp.max(gpick, axis=1, keepdims=True)
+    columns = jnp.where(wide == 0, pick, jnp.where(wide == 2, gpick, 0))
+    keys[0:OWN] = jnp.where(wide[:OWN] == 1, inverse, columns[:OWN])
+    keys[OWN : OWNERS * RANKS] = columns[OWN:]
+    keys[OWNERS * RANKS :] = jnp.zeros((2 * OWN - OWNERS * RANKS, OWN), jnp.int32)
+    rows[:, :OWN] = keys[:OWN].T[:8]
+    rows[:, OWN:] = keys[OWN:].T[:8]
     rows[3:4, :OWN] = my_code
-    rows[3:4, OWN:] = my_code
     load_lists = pltpu.make_async_copy(rows, lists, ld.at[7])
     load_lists.start()
 
+    load_own.wait()
+    load_lists.wait()
+    my_rows = pl.ds(me * RANKS, RANKS)
+
+    def tp_of(dz, dy):
+        return lax.rem(lax.rem(z + dz, 8), 4) * 4 + lax.rem(y + dy, 4)
+
+    def pick_tiles(m):
+        @pl.loop(0, OWNERS)
+        def _(t):
+            for k in range(RANKS):
+                outg[m, t * RANKS + k] = own[m, lists[0, t * RANKS + k]]
+
+    def send_tiles(m):
+        for n, (mm, dz, dy) in enumerate(SENT):
+            if mm == m:
+                rows_of = pl.ds(tp_of(dz, dy) * RANKS, RANKS)
+                send(outg.at[m, rows_of], arrv[m].at[my_rows], a_s.at[n], a_r.at[n], dev(dz, dy))
+
+    phase("p02_pick0")
+    pick_tiles(0)
     phase("p02_barrier")
     pl.semaphore_wait(barrier, 34)
+    phase("p03_pick_send")
+    send_tiles(0)
+    pick_tiles(1)
+    send_tiles(1)
     load_cot.start()
     load_tok.wait()
 
+    pair = zl + 1 - 2 * lax.rem(zl, 2)
+    cross = lax.rem(zl + 2, 4)
+
     def zq_of(q):
-        return lax.rem(zl + 4 - q, 4)
+        return (zl, pair, cross, 3 - zl)[q]
+
+    def at_z(to):
+        return (to, y, zh, x, c)
 
     def near_tokens(q):
-        block = xs.at[zq_of(q), y]
-        for way, dy in ((0, 1), (1, 3)):
-            send(block, block, tn_s.at[q, way], tn_r.at[q, way], dev(dy=dy))
+        for part_of in range(2):
+            for way in range(2):
+                h = way if part_of == 0 else 1 - way
+                block = xs.at[zq_of(q), y, pl.ds(16 * h, 16)]
+                send(block, block, tn_s.at[q, way, h], tn_r.at[q, way, h], y_to[way])
 
     def far_tokens(q):
-        for way, dy in ((0, 1), (1, 3)):
-            src = lax.rem(y + 4 - dy, 4)
-            recv(xs.at[zq_of(q), src], tn_s.at[q, way], tn_r.at[q, way])
+        phase(f"p08_far{q}")
+        for way in range(2):
+            src = lax.rem(y + (3 if way == 0 else 1), 4)
             half = xs.at[zq_of(q), src, pl.ds(16 * way, 16)]
-            send(half, half, tf_s.at[q, way], tf_r.at[q, way], dev(dy=dy))
+            recv(half, tn_s.at[q, way, way], tn_r.at[q, way, way])
+            send(half, half, tf_s.at[q, way], tf_r.at[q, way], y_to[way])
 
     def last_tokens(q):
-        src = lax.rem(y + 2, 4)
-        for way in range(2):
-            recv(xs.at[zq_of(q), src, pl.ds(16 * way, 16)], tf_s.at[q, way], tf_r.at[q, way])
-
+        phase(f"p14_last{q}")
+        for way in range(2):
+            src, h = lax.rem(y + (3 if way == 0 else 1), 4), 1 - way
+            recv(xs.at[zq_of(q), src, pl.ds(16 * h, 16)], tn_s.at[q, way, h], tn_r.at[q, way, h])
+            recv(xs.at[zq_of(q), lax.rem(y + 2, 4), pl.ds(16 * way, 16)], tf_s.at[q, way], tf_r.at[q, way])
+
+    x_to = (dev(dx=1), dev(dx=3))
+    y_to = (dev(dy=1), dev(dy=3))
     near_tokens(0)
 
-    phase("p03_pick_send")
-    load_lists.wait()
-    load_own.wait()
-    my_rows = pl.ds(me * RANKS, RANKS)
-
-    def tp_of(dz, dy):
-        return lax.rem(lax.rem(z + dz, 8), 4) * 4 + lax.rem(y + dy, 4)
-
-    def pick_into(dst, m, t):
-        @pl.loop(0, RANKS)
-        def _(k):
-            dst[t * RANKS + k] = own[m, lists[0, t * RANKS + k]]
-
-    for n, (m, dz, dy) in enumerate(SENT):
-        t = tp_of(dz, dy)
-        pick_into(outg.at[m], m, t)
-        send(outg.at[m, pl.ds(t * RANKS, RANKS)], arrv[m].at[my_rows], a_s.at[n], a_r.at[n], dev(dz, dy))
     for m in range(2):
-        pick_into(arrv[m], m, me)
+        for k in range(RANKS):
+            arrv[m][me * RANKS + k] = own[m, lists[0, me * RANKS + k]]
 
     phase("p04_tokz")
-    for j in (1, 3, 2):
-        to = (lax.rem(zl + j, 4), y, zh, x, c)
-        send(xs.at[zl, y], xs.at[zl, y], tz_s.at[j - 1], tz_r.at[j - 1], to)
+    for i, to in enumerate((pair, cross)):
+        send(xs.at[zl, y], xs.at[zl, y], tz_s.at[i], tz_r.at[i], at_z(to))
 
     def side_band(way, core):
         return lax.rem(x + (3 if way == 0 else 1), 4) * 2 + core
 
     far_x = lax.rem(x + 2, 4) * 2
-    x_to = (dev(dx=1), dev(dx=3))
-    y_to = (dev(dy=1), dev(dy=3))
 
     def own_weights(m):
         phase(f"p05_wait_a2a{m}")
@@ -241,57 +253,63 @@
 
     def tokens_z(q):
         phase(f"p07_tokz{q}")
-        recv(xs.at[zq_of(q), y], tz_s.at[q - 1], tz_r.at[q - 1])
+        block = xs.at[zq_of(q), y]
+        recv(block, tz_s.at[q - 1], tz_r.at[q - 1])
+        if q == 2:
+            send(block, block, tz_s.at[2], tz_r.at[2], at_z(pair))
         near_tokens(q)
 
     own_weights(0)
     own_weights(1)
-    phase("p08_far0")
+    near_weights(0)
     far_tokens(0)
     tokens_z(1)
+    tokens_z(2)
+    far_tokens(1)
     tokens_z(3)
-    near_weights(0)
-    tokens_z(2)
-    phase("p10_far1")
-    far_tokens(1)
     near_weights(1)
-    phase("p10_far3")
+    far_tokens(2)
+    far_weights(0)
     far_tokens(3)
-    far_weights(0)
-    phase("p10_far2")
-    far_tokens(2)
     far_weights(1)
+    last_tokens(0)
+    last_tokens(1)
     partner_weights(0)
     partner_weights(1)
-    phase("p14_lasttok")
-    for q in (0, 1, 3, 2):
-        last_tokens(q)
-
-    phase("p16_fwd")
-
-    @pl.loop(0, 4)
-    def _(k):
-        cols = pl.ds(pl.multiple_of(k * 1024, 1024), 1024)
-        a = xs[:, :, :, cols].reshape(GROUP, 1024)
-        for m in range(2):
-            w = ws[m, pl.ds(k * 8, 8)].reshape(1024, GROUP)
-            v = jnp.dot(a, w, preferred_element_type=F32)
-
-            @pl.when(k == 0)
-            def _():
-                acc[m] = v
-
-            @pl.when(k > 0)
-            def _():
-                acc[m] += v
-
+
+    def forward(qa, qb):
+        phase(f"p16_fwd{qa}")
+        za, zb = zq_of(qa), zq_of(qb)
+
+        @pl.loop(0, 4)
+        def _(k):
+            cols = pl.ds(pl.multiple_of(k * 1024, 1024), 1024)
+            a = jnp.concatenate([xs[zz, :, :, cols].reshape(128, 1024) for zz in (za, zb)], axis=0)
+            for m in range(2):
+                w = ws[m, pl.ds(k * 8, 8)].reshape(1024, GROUP)
+                v = jnp.dot(a, w, preferred_element_type=F32)
+
+                @pl.when(k == 0)
+                def _():
+                    acc[m, za], acc[m, zb] = v[:128], v[128:]
+
+                @pl.when(k > 0)
+                def _():
+                    acc[m, za] += v[:128]
+                    acc[m, zb] += v[128:]
+
+    forward(0, 1)
+    last_tokens(2)
+    last_tokens(3)
+    forward(2, 3)
     phase("p17_elem")
     load_cot.wait()
 
     @pl.loop(0, 16)
     def _(i):
         rows_of = pl.ds(pl.multiple_of(i * 32, 32), 32)
-        gate, up = acc[0, rows_of], acc[1, rows_of]
+        at = (lax.div(i, 4), pl.ds(pl.multiple_of(lax.rem(i, 4) * 32, 32), 32))
+        gate, up = acc[0, *at], acc[1, *at]
         s = jax.nn.sigmoid(gate)
         act = gate * s
         ct = cot[rows_of].astype(F32)
@@ -365,45 +383,61 @@
             for way in range(2):
                 total += ynear[st, way, h].astype(F32)
             term[st, y, h] = total.astype(BF)
-        for j in range(1, 4):
-            zt = lax.rem(zl + j, 4)
-            send(
-                term.at[st, y, lax.div(zt, 2), lax.rem(zt, 2)], zrecv.at[st, j - 1],
-                zr_s.at[st, j - 1], zr_r.at[st, j - 1], (zt, y, zh, x, c),
-            )
+        send(
+            term.at[st, y, :, lax.rem(pair, 2)], zpair.at[st], zr_s.at[st, 0], zr_r.at[st, 0], at_z(pair)
+        )
+
+    high_z, low_z = lax.div(zl, 2), lax.rem(zl, 2)
+
+    def z_pass(st):
+        phase(f"p26_zpass{st}")
+        recv(zpair.at[st], zr_s.at[st, 0], zr_r.at[st, 0])
+        here = term[st, y, 1 - high_z, low_z].astype(F32)
+        term[st, y, 1 - high_z, low_z] = (here + zpair[st, 1 - high_z].astype(F32)).astype(BF)
+        send(
+            term.at[st, y, 1 - high_z, low_z], zcross.at[st], zr_s.at[st, 1], zr_r.at[st, 1], at_z(cross)
+        )
 
     highs = (1 - zh, zh)
     mat = part.at[c]
 
-    def partner_sum(k):
-        phase(f"p22_partner{k}")
+    def partner_send(k, h):
         for i in range(4):
-            recv(precv.at[xt[i], highs[k]], pd_s.at[k, i], pd_r.at[k, i])
-            for h in range(2):
-
-                @pl.loop(0, 4)
-                def _(r):
-                    at = (xt[i], highs[k], h, pl.ds(r * 4, 4))
-                    mat[at] = (mat[at].astype(F32) + precv[at].astype(F32)).astype(BF)
-
-    def x_args(k):
-        a = lambda t, h: mat.at[t, highs[k], h]
-        return a, xt, xfar.at[k], xnear.at[k], xf_s.at[k], xf_r.at[k], xn_s.at[k], xn_r.at[k], x_to
-
-    def x_open(k):
-        ring_open(*x_args(k))
-
-    def x_pass(k):
-        phase(f"p24_xpass{k}")
-
-        def add(t, way):
+            send(
+                part.at[other, xt[i], highs[k], h], precv.at[xt[i], highs[k], h],
+                pd_s.at[k, i, h], pd_r.at[k, i, h], dev(dc=1),
+            )
+
+    def partner_sum(k, h):
+        phase(f"p22_partner{k}{h}")
+        for i in range(4):
+            recv(precv.at[xt[i], highs[k], h], pd_s.at[k, i, h], pd_r.at[k, i, h])
+
             @pl.loop(0, 4)
             def _(r):
-                rs = pl.ds(r * 4, 4)
-                at = (t, highs[k], way, rs)
-                mat[at] = (mat[at].astype(F32) + xfar[k, way, rs].astype(F32)).astype(BF)
-
-        ring_pass(*x_args(k), add)
+                at = (xt[i], highs[k], h, pl.ds(r * 4, 4))
+                mat[at] = (mat[at].astype(F32) + precv[at].astype(F32)).astype(BF)
+
+    def x_far(k, way):
+        send(mat.at[xt[0], highs[k], way], xfar.at[k, way], xf_s.at[k, way], xf_r.at[k, way], x_to[way])
+
+    def x_near(k, way, h):
+        send(
+            mat.at[xt[1 + way], highs[k], h], xnear.at[k, way, h], xn_s.at[k, way, h], xn_r.at[k, way, h],
+            x_to[way],
+        )
+
+    def x_pass(k, way):
+        phase(f"p24_xpass{k}{way}")
+        recv(xfar.at[k, way], xf_s.at[k, way], xf_r.at[k, way])
+
+        @pl.loop(0, 4)
+        def _(r):
+            rs = pl.ds(r * 4, 4)
+            at = (xt[1 + way], highs[k], way, rs)
+            mat[at] = (mat[at].astype(F32) + xfar[k, way, rs].astype(F32)).astype(BF)
+
+        x_near(k, way, way)
 
     def x_close(k):
         phase(f"p27_xclose{k}")
@@ -438,62 +472,71 @@
                         g_s.at[k, n], g_r.at[k, n], to,
                     )
 
+    def products(half):
+        phase(f"p18_dw{half}")
+
+        @pl.loop(0, 4)
+        def _(d):
+            cols = pl.ds(pl.multiple_of(half * (D // 2) + d * 512, 512), 512)
+            a = xs[:, :, :, cols].reshape(GROUP, 512)
+            v = lax.dot_general(a, grads[...], (((0,), (0,)), ((), ())), preferred_element_type=F32)
+            v = v.astype(BF).reshape(4, 2, 4, 16, 1024)
+            for m in range(2):
+                for xx in range(4):
+                    for col in range(CPD):
+                        lo = m * GROUP + col * TILE
+                        for high in range(2):
+                            part[m, xx, high, half, pl.ds(d * 4, 4), col] = v[:, high, xx, :, lo : lo + TILE]
+
+        partner_send(0, half)
+
+    products(0)
     share(0)
     y_open(0)
-
-    phase("p18_dw")
-
-    @pl.loop(0, 8)
-    def _(d):
-        cols = pl.ds(pl.multiple_of(d * 512, 512), 512)
-        a = xs[:, :, :, cols].reshape(GROUP, 512)
-        v = lax.dot_general(a, grads[...], (((0,), (0,)), ((), ())), preferred_element_type=F32)
-        v = v.astype(BF).reshape(4, 2, 4, 16, 1024)
-        half, row = lax.div(d, 4), lax.rem(d, 4) * 4
-        for m in range(2):
-            for xx in range(4):
-                for col in range(CPD):
-                    lo = m * GROUP + col * TILE
-                    for high in range(2):
-                        part[m, xx, high, half, pl.ds(row, 4), col] = v[:, high, xx, :, lo : lo + TILE]
-
-    for k in range(2):
-        for i in range(4):
-            send(
-                part.at[other, xt[i], highs[k]], precv.at[xt[i], highs[k]],
-                pd_s.at[k, i], pd_r.at[k, i], dev(dc=1),
-            )
-
+    partner_sum(0, 0)
+    x_far(0, 0)
+    x_near(0, 1, 0)
+    partner_send(1, 0)
+    products(1)
     y_pass(0)
     share(1)
     y_open(1)
-    partner_sum(0)
-    x_open(0)
+    partner_sum(0, 1)
+    x_near(0, 0, 1)
+    x_far(0, 1)
+    partner_send(1, 1)
     share(2)
+    y_close(0)
     share(3)
-    partner_sum(1)
+    x_pass(0, 0)
+    partner_sum(1, 0)
+    partner_sum(1, 1)
     y_pass(1)
     y_open(2)
-    y_close(0)
-    x_pass(0)
-    x_open(1)
+    x_pass(0, 1)
+    for way in range(2):
+        x_far(1, way)
+        x_near(1, way, 1 - way)
+    z_pass(0)
     y_close(1)
     y_pass(2)
     y_open(3)
+    x_close(0)
+    x_pass(1, 0)
+    z_pass(1)
     y_close(2)
-    x_close(0)
+    x_pass(1, 1)
     y_pass(3)
-    x_pass(1)
     y_close(3)
     x_close(1)
+    z_pass(2)
+    z_pass(3)
 
     phase("p30_zrecv")
     for st in range(STAGES):
-        for j in range(1, 4):
-            recv(zrecv.at[st, j - 1], zr_s.at[st, j - 1], zr_r.at[st, j - 1])
-        total = term[st, y, lax.div(zl, 2), lax.rem(zl, 2)].astype(F32)
-        for j in range(3):
-            total += zrecv[st, j].astype(F32)
+        recv(zcross.at[st], zr_s.at[st, 1], zr_r.at[st, 1])
+        total = term[st, y, high_z, low_z].astype(F32) + zpair[st, high_z].astype(F32)
+        total += zcross[st].astype(F32)
         dnout[:, st * COLS : (st + 1) * COLS] = total.astype(BF)
 
     store_dn = pltpu.make_async_copy(dnout, dn_hbm, ld.at[4])
@@ -533,10 +576,23 @@
     phase(None)
 
 
+def hand_over(a, b, c, a_out, b_out, c_out, a_mid, b_mid, c_mid, sems):
+    pairs = ((c, c_mid, c_out), (a, a_mid, a_out), (b, b_mid, b_out))
+    loads = [pltpu.make_async_copy(src, mid, sems.at[i]) for i, (src, mid, _) in enumerate(pairs)]
+    stores = [pltpu.make_async_copy(mid, dst, sems.at[3 + i]) for i, (_, mid, dst) in enumerate(pairs)]
+    for load in loads:
+        load.start()
+    for load, store in zip(loads, stores):
+        load.wait()
+        store.start()
+    for store in stores:
+        store.wait()
+
+
 def step(normed, cotangent, weight_tiles, slot_tile):
     dma = pltpu.SemaphoreType.DMA
     scratch = [
-        pltpu.VMEM((OWN, OWN), jnp.int32),
+        pltpu.VMEM((2 * OWN, OWN), jnp.int32),
         pltpu.VMEM((8, 2 * OWN), jnp.int32),
         pltpu.SMEM((8, 2 * OWN), jnp.int32),
         pltpu.VMEM((2, OWN, 16, TILE), BF),
@@ -547,12 +603,13 @@
         pltpu.VMEM((2, 32, 8, 16, GROUP), BF),
         pltpu.VMEM((GROUP, GROUP), BF),
         pltpu.VMEM((GROUP, GROUP), BF),
-        pltpu.VMEM((2, GROUP, GROUP), F32),
+        pltpu.VMEM((2, 4, 128, GROUP), F32),
         pltpu.VMEM((GROUP, 2 * GROUP), BF),
         pltpu.VMEM((STAGES, 4, 2, 2, TOK, COLS), BF),
         pltpu.VMEM((STAGES, 2, 2, TOK, COLS), BF),
         pltpu.VMEM((STAGES, 2, 2, 2, TOK, COLS), BF),
-        pltpu.VMEM((STAGES, 3, TOK, COLS), BF),
+        pltpu.VMEM((STAGES, 2, TOK, COLS), BF),
+        pltpu.VMEM((STAGES, TOK, COLS), BF),
         pltpu.VMEM((TOK, D), BF),
         pltpu.VMEM((2, 4, 2, 2, 16, 4, 16, TILE), BF),
         pltpu.VMEM((4, 2, 2, 16, 4, 16, TILE), BF),
@@ -566,18 +623,19 @@
         dma((8,)),
     ]
     for shape in (
-        (len(SENT),), (3,), (4, 2), (4, 2), (2, 2), (2, 2), (2, 5), (2, 4), (2, 2), (2, 2, 2),
-        (STAGES, 2), (STAGES, 2, 2), (STAGES, 3), (2, 16), (1,),
+        (len(SENT),), (3,), (4, 2, 2), (4, 2), (2, 2), (2, 2), (2, 5), (2, 4, 2), (2, 2), (2, 2, 2),
+        (STAGES, 2), (STAGES, 2, 2), (STAGES, 2), (2, 16), (1,),
     ):
         scratch += [dma(shape), dma(shape)]
     anywhere = pl.BlockSpec(memory_space=pl.ANY)
-    return pl.pallas_call(
+    out_shape = (
+        jax.ShapeDtypeStruct((GROUP, GROUP), BF),
+        jax.ShapeDtypeStruct((TOK, D), BF),
+        jax.ShapeDtypeStruct((2, OWN, 8, TILE), F32),
+    )
+    results = pl.pallas_call(
         kernel,
-        out_shape=(
-            jax.ShapeDtypeStruct((GROUP, GROUP), BF),
-            jax.ShapeDtypeStruct((TOK, D), BF),
-            jax.ShapeDtypeStruct((2, OWN, 8, TILE), F32),
-        ),
+        out_shape=out_shape,
         in_specs=[pl.BlockSpec(memory_space=pltpu.VMEM)] + [anywhere] * 3,
         out_specs=[anywhere] * 3,
         scratch_shapes=scratch,
@@ -586,6 +644,14 @@
         ),
         name="gated_pair",
     )(slot_tile.reshape(OWNERS, OWN), normed, cotangent, weight_tiles)
+    return pl.pallas_call(
+        hand_over,
+        out_shape=out_shape,
+        in_specs=[anywhere] * 3,
+        out_specs=[anywhere] * 3,
+        scratch_shapes=[pltpu.VMEM(o.shape, o.dtype) for o in out_shape] + [dma((6,))],
+        name="hand_over",
+    )(*results)
 
 
 def solution(mesh):

time: 161 us -> 150 us (0.932)
  local copies, waits for them, and re-layouts: 5.8 us -> 0 us
  Pallas kernels: 154 us -> 149 us
    unnamed x3 -> x0, local copies, waits for them, and re-layouts: 5.8 us -> none
    pallas_call x1 -> x2, Pallas kernels: 154 us -> 149 us  [the longest x1 146 us: step(): pl.pallas_call(kernel, out_shape=out_shape, in_specs=[pl.BlockSpec(memory...]
where the time goes in v3:
time: 150 us; the launch traced here: 149 us
  Pallas kernels  149 us (99%)
    pallas_call x1, Pallas kernels, step(): pl.pallas_call(kernel, out_shape=out_shape, in_specs=[pl.BlockSpec(memory...  146 us

profile of v3, /device:TPU:1, one launch (start us, length us, event | category | flops | bytes accessed | tf_op | source)
XLA Modules:
  0.0 149.5 jit_solution(14822481894460006051)
XLA Ops:
  0.6 146.3 %gated_pair.1 = (bf16[512,512]{1,0:T(8,128)(2,1)}, bf16[32,4096]{1,0:T(8,128)(2,1)}, f32[2,128,8,128]{3,2,1,0:T(8,128)}) custom-call(s32[16,128]{1,0:T(8,128)} %bitcast.1, bf16[32,4096]{1,0:T(8,128)(2,1)} %tok_hbm.1, bf16[512,512]{1,0:T(8,128)(2,1)} %cot_hbm.1, bf16[2,128,128,128]{3,2,1,0:T(8,128)(2,1)} %own_hbm.1), custom_call_target="tpu_custom_call" | custom-call | tf_op jit(solution)/shard_map/gated_pair/pallas_call | solution.py:636
  147.0 2.5 %hand_over.1 = (bf16[512,512]{1,0:T(8,128)(2,1)}, bf16[32,4096]{1,0:T(8,128)(2,1)}, f32[2,128,8,128]{3,2,1,0:T(8,128)}) custom-call(bf16[512,512]{1,0:T(8,128)(2,1)} %get-tuple-element.6.a, bf16[32,4096]{1,0:T(8,128)(2,1)} %get-tuple-element.7.b, f32[2,128,8,128]{3,2,1,0:T(8,128)} %get-tuple-element.8.c), custom_call_target="tpu_custom_call" | custom-call | tf_op jit(solution)/shard_map/hand_over/pallas_call | solution.py:647

commit v4 on v3

--- a/solution.py
+++ b/solution.py
@@ -31,7 +31,7 @@
 def kernel(
     tiles_ref, tok_hbm, cot_hbm, own_hbm,
     hid_hbm, dn_hbm, gt_hbm,
-    keys, rows, lists, own, outg, arrv_a, arrv_b, xs, ws, cot, hid, acc, grads, term, yfar, ynear, zpair, zcross, dnout,
+    keys, rows, lists, own, outg, arrv_a, arrv_b, xs, ws, cot, hid, acc, grads, term, yfar, ynear, zpair, zcross, zdirect, dnout,
     part, precv, xfar, xnear, fsum, gout, garr, give, gres,
     ld, a_s, a_r, tz_s, tz_r, tn_s, tn_r, tf_s, tf_r, wn_s, wn_r, wf_s, wf_r, wd_s, wd_r,
     pd_s, pd_r, xf_s, xf_r, xn_s, xn_r, yf_s, yf_r, yn_s, yn_r, zr_s, zr_r, g_s, g_r, q_s, q_r,
@@ -259,6 +259,29 @@
             send(block, block, tz_s.at[2], tz_r.at[2], at_z(pair))
         near_tokens(q)
 
+    high_z, low_z = lax.div(zl, 2), lax.rem(zl, 2)
+
+    def forward(t, matrices):
+        phase(f"p16_fwd{t}{matrices[0]}")
+        hh = high_z if t == 0 else 1 - high_z
+        rows_of = pl.ds(pl.multiple_of(hh * (GROUP // 2), GROUP // 2), GROUP // 2)
+
+        @pl.loop(0, 4)
+        def _(k):
+            cols = pl.ds(pl.multiple_of(k * 1024, 1024), 1024)
+            a = xs[pl.ds(hh * 2, 2), :, :, cols].reshape(GROUP // 2, 1024)
+            for m in matrices:
+                w = ws[m, pl.ds(k * 8, 8)].reshape(1024, GROUP)
+                v = jnp.dot(a, w, preferred_element_type=F32)
+
+                @pl.when(k == 0)
+                def _():
+                    acc[m, rows_of] = v
+
+                @pl.when(k > 0)
+                def _():
+                    acc[m, rows_of] += v
+
     own_weights(0)
     own_weights(1)
     near_weights(0)
@@ -270,46 +293,24 @@
     near_weights(1)
     far_tokens(2)
     far_weights(0)
-    far_tokens(3)
-    far_weights(1)
     last_tokens(0)
     last_tokens(1)
     partner_weights(0)
+    forward(0, (0,))
+    far_tokens(3)
+    far_weights(1)
     partner_weights(1)
-
-    def forward(qa, qb):
-        phase(f"p16_fwd{qa}")
-        za, zb = zq_of(qa), zq_of(qb)
-
-        @pl.loop(0, 4)
-        def _(k):
-            cols = pl.ds(pl.multiple_of(k * 1024, 1024), 1024)
-            a = jnp.concatenate([xs[zz, :, :, cols].reshape(128, 1024) for zz in (za, zb)], axis=0)
-            for m in range(2):
-                w = ws[m, pl.ds(k * 8, 8)].reshape(1024, GROUP)
-                v = jnp.dot(a, w, preferred_element_type=F32)
-
-                @pl.when(k == 0)
-                def _():
-                    acc[m, za], acc[m, zb] = v[:128], v[128:]
-
-                @pl.when(k > 0)
-                def _():
-                    acc[m, za] += v[:128]
-                    acc[m, zb] += v[128:]
-
-    forward(0, 1)
+    forward(0, (1,))
     last_tokens(2)
     last_tokens(3)
-    forward(2, 3)
+    forward(1, (0, 1))
     phase("p17_elem")
     load_cot.wait()
 
     @pl.loop(0, 16)
     def _(i):
         rows_of = pl.ds(pl.multiple_of(i * 32, 32), 32)
-        at = (lax.div(i, 4), pl.ds(pl.multiple_of(lax.rem(i, 4) * 32, 32), 32))
-        gate, up = acc[0, *at], acc[1, *at]
+        gate, up = acc[0, rows_of], acc[1, rows_of]
         s = jax.nn.sigmoid(gate)
         act = gate * s
         ct = cot[rows_of].astype(F32)
@@ -383,11 +384,17 @@
             for way in range(2):
                 total += ynear[st, way, h].astype(F32)
             term[st, y, h] = total.astype(BF)
-        send(
-            term.at[st, y, :, lax.rem(pair, 2)], zpair.at[st], zr_s.at[st, 0], zr_r.at[st, 0], at_z(pair)
-        )
-
-    high_z, low_z = lax.div(zl, 2), lax.rem(zl, 2)
+        if st < 2:
+            send(
+                term.at[st, y, :, lax.rem(pair, 2)], zpair.at[st], zr_s.at[st, 0], zr_r.at[st, 0], at_z(pair)
+            )
+            return
+        for j in range(1, 4):
+            zt = lax.rem(zl + j, 4)
+            send(
+                term.at[st, y, lax.div(zt, 2), lax.rem(zt, 2)], zdirect.at[st - 2, j - 1],
+                zr_s.at[st, j - 1], zr_r.at[st, j - 1], at_z(zt),
+            )
 
     def z_pass(st):
         phase(f"p26_zpass{st}")
@@ -401,8 +408,11 @@
     highs = (1 - zh, zh)
     mat = part.at[c]
 
+    def pieces(h):
+        return (0, 2 - h, 1 + h, 3)
+
     def partner_send(k, h):
-        for i in range(4):
+        for i in pieces(h):
             send(
                 part.at[other, xt[i], highs[k], h], precv.at[xt[i], highs[k], h],
                 pd_s.at[k, i, h], pd_r.at[k, i, h], dev(dc=1),
@@ -410,13 +420,18 @@
 
     def partner_sum(k, h):
         phase(f"p22_partner{k}{h}")
-        for i in range(4):
+        for n, i in enumerate(pieces(h)):
             recv(precv.at[xt[i], highs[k], h], pd_s.at[k, i, h], pd_r.at[k, i, h])
 
             @pl.loop(0, 4)
             def _(r):
                 at = (xt[i], highs[k], h, pl.ds(r * 4, 4))
                 mat[at] = (mat[at].astype(F32) + precv[at].astype(F32)).astype(BF)
+
+            if k == 0 and n == 0:
+                x_far(0, h)
+            if k == 0 and n == 1:
+                x_near(0, 1 - h, h)
 
     def x_far(k, way):
         send(mat.at[xt[0], highs[k], way], xfar.at[k, way], xf_s.at[k, way], xf_r.at[k, way], x_to[way])
@@ -494,17 +509,13 @@
     share(0)
     y_open(0)
     partner_sum(0, 0)
-    x_far(0, 0)
-    x_near(0, 1, 0)
     partner_send(1, 0)
     products(1)
+    share(1)
+    partner_sum(0, 1)
+    partner_send(1, 1)
     y_pass(0)
-    share(1)
     y_open(1)
-    partner_sum(0, 1)
-    x_near(0, 0, 1)
-    x_far(0, 1)
-    partner_send(1, 1)
     share(2)
     y_close(0)
     share(3)
@@ -519,24 +530,28 @@
         x_near(1, way, 1 - way)
     z_pass(0)
     y_close(1)
+    x_close(0)
     y_pass(2)
     y_open(3)
-    x_close(0)
     x_pass(1, 0)
     z_pass(1)
     y_close(2)
     x_pass(1, 1)
     y_pass(3)
+    x_close(1)
     y_close(3)
-    x_close(1)
-    z_pass(2)
-    z_pass(3)
 
     phase("p30_zrecv")
     for st in range(STAGES):
-        recv(zcross.at[st], zr_s.at[st, 1], zr_r.at[st, 1])
-        total = term[st, y, high_z, low_z].astype(F32) + zpair[st, high_z].astype(F32)
-        total += zcross[st].astype(F32)
+        total = term[st, y, high_z, low_z].astype(F32)
+        if st < 2:
+            recv(zcross.at[st], zr_s.at[st, 1], zr_r.at[st, 1])
+            total += zpair[st, high_z].astype(F32)
+            total += zcross[st].astype(F32)
+        else:
+            for j in range(3):
+                recv(zdirect.at[st - 2, j], zr_s.at[st, j], zr_r.at[st, j])
+                total += zdirect[st - 2, j].astype(F32)
         dnout[:, st * COLS : (st + 1) * COLS] = total.astype(BF)
 
     store_dn = pltpu.make_async_copy(dnout, dn_hbm, ld.at[4])
@@ -603,13 +618,14 @@
         pltpu.VMEM((2, 32, 8, 16, GROUP), BF),
         pltpu.VMEM((GROUP, GROUP), BF),
         pltpu.VMEM((GROUP, GROUP), BF),
-        pltpu.VMEM((2, 4, 128, GROUP), F32),
+        pltpu.VMEM((2, GROUP, GROUP), F32),
         pltpu.VMEM((GROUP, 2 * GROUP), BF),
         pltpu.VMEM((STAGES, 4, 2, 2, TOK, COLS), BF),
         pltpu.VMEM((STAGES, 2, 2, TOK, COLS), BF),
         pltpu.VMEM((STAGES, 2, 2, 2, TOK, COLS), BF),
-        pltpu.VMEM((STAGES, 2, TOK, COLS), BF),
-        pltpu.VMEM((STAGES, TOK, COLS), BF),
+        pltpu.VMEM((2, 2, TOK, COLS), BF),
+        pltpu.VMEM((2, TOK, COLS), BF),
+        pltpu.VMEM((2, 3, TOK, COLS), BF),
         pltpu.VMEM((TOK, D), BF),
         pltpu.VMEM((2, 4, 2, 2, 16, 4, 16, TILE), BF),
         pltpu.VMEM((4, 2, 2, 16, 4, 16, TILE), BF),
@@ -624,7 +640,7 @@
     ]
     for shape in (
         (len(SENT),), (3,), (4, 2, 2), (4, 2), (2, 2), (2, 2), (2, 5), (2, 4, 2), (2, 2), (2, 2, 2),
-        (STAGES, 2), (STAGES, 2, 2), (STAGES, 2), (2, 16), (1,),
+        (STAGES, 2), (STAGES, 2, 2), (STAGES, 3), (2, 16), (1,),
     ):
         scratch += [dma(shape), dma(shape)]
     anywhere = pl.BlockSpec(memory_space=pl.ANY)

time: 150 us -> 149 us (level)
  no operation moved by 1% of the time
where the time goes in v4:
time: 149 us; the launch traced here: 148 us
  Pallas kernels  148 us (99%)
    pallas_call x1, Pallas kernels, step(): pl.pallas_call(kernel, out_shape=out_shape, in_specs=[pl.BlockSpec(memory...  145 us

profile of v4, /device:TPU:1, one launch (start us, length us, event | category | flops | bytes accessed | tf_op | source)
XLA Modules:
  0.0 148.4 jit_solution(9260670813154876113)
XLA Ops:
  0.6 145.2 %gated_pair.1 = (bf16[512,512]{1,0:T(8,128)(2,1)}, bf16[32,4096]{1,0:T(8,128)(2,1)}, f32[2,128,8,128]{3,2,1,0:T(8,128)}) custom-call(s32[16,128]{1,0:T(8,128)} %bitcast.1, bf16[32,4096]{1,0:T(8,128)(2,1)} %tok_hbm.1, bf16[512,512]{1,0:T(8,128)(2,1)} %cot_hbm.1, bf16[2,128,128,128]{3,2,1,0:T(8,128)(2,1)} %own_hbm.1), custom_call_target="tpu_custom_call" | custom-call | tf_op jit(solution)/shard_map/gated_pair/pallas_call | solution.py:652
  145.9 2.5 %hand_over.1 = (bf16[512,512]{1,0:T(8,128)(2,1)}, bf16[32,4096]{1,0:T(8,128)(2,1)}, f32[2,128,8,128]{3,2,1,0:T(8,128)}) custom-call(bf16[512,512]{1,0:T(8,128)(2,1)} %get-tuple-element.6.a, bf16[32,4096]{1,0:T(8,128)(2,1)} %get-tuple-element.7.b, f32[2,128,8,128]{3,2,1,0:T(8,128)} %get-tuple-element.8.c), custom_call_target="tpu_custom_call" | custom-call | tf_op jit(solution)/shard_map/hand_over/pallas_call | solution.py:663
